TPU v7x, 128 devices: a whole 4x4x4 slice. The times are simulated.
128 devices in a mesh: rep: 16 (over z, y), nodes: 8 (over x, core).
Axes of the slice: x: 4, y: 4, z: 4, core: 2. Of those that a mesh axis runs over, the one named last changes fastest.
Arguments:
- adjacency: bfloat16 [16, 1536, 24576], P(None, 'nodes', 'rep')
- features: bfloat16 [24576, 128], P(('rep', 'nodes'))
- w_one: float32 [128, 256], replicated
- w_two: float32 [256, 40], replicated
- labels: int32 [24576], P(('rep', 'nodes'))
- label_mask: int32 [24576], P(('rep', 'nodes'))
Outputs:
- output 1: float32 [], replicated
- output 2: float32 [128, 256], replicated
- output 3: float32 [256, 40], replicated
All inputs are finite; a program needn't handle non-finite values.
Results may differ from a plain program's by a relative error of at most 0.001.
Values are sent between devices in bfloat16 or wider.
A program may use at most 1 GiB of HBM per device.

v0:
```python
import jax
import jax.numpy as jnp
from jax import lax
from jax.sharding import PartitionSpec as P


def solution(mesh):
    all_axes = ("rep", "nodes")
    row_spec = P(("rep", "nodes"))

    def device_step(adj_blk, feat_blk, w_one, w_two, label_blk, mask_blk):
        n_class = w_two.shape[1]
        w_one_lo = w_one.astype(jnp.bfloat16)
        w_two_lo = w_two.astype(jnp.bfloat16)

        def spread(y_blk):
            gathered = lax.all_gather(y_blk, "nodes", axis=0, tiled=True)
            part_sum = lax.dot_general(adj_blk, gathered, (((2,), (0,)), ((), ())), preferred_element_type=jnp.float32)
            return lax.psum_scatter(part_sum, "rep", scatter_dimension=0, tiled=False)

        def collect(g_blk):
            gathered = lax.all_gather(g_blk, "rep", axis=0)
            part_sum = lax.dot_general(adj_blk, gathered, (((0, 1), (0, 1)), ((), ())), preferred_element_type=jnp.float32)
            return lax.psum_scatter(part_sum, "nodes", scatter_dimension=0, tiled=True)

        y_one = jnp.dot(feat_blk, w_one_lo, preferred_element_type=jnp.float32).astype(jnp.bfloat16)
        z_one = spread(y_one)
        h_one = jnp.maximum(z_one, 0.0).astype(jnp.bfloat16)
        y_two = jnp.dot(h_one, w_two_lo, preferred_element_type=jnp.float32).astype(jnp.bfloat16)
        z_two = spread(y_two)
        weights = mask_blk.astype(jnp.float32)
        log_probs = jax.nn.log_softmax(z_two, axis=-1)
        one_hot = (label_blk[:, None] == jnp.arange(n_class)[None, :]).astype(jnp.float32)
        local_sums = jnp.stack([jnp.sum(weights), -jnp.sum(weights * jnp.sum(one_hot * log_probs, axis=-1))])
        global_sums = lax.psum(local_sums, all_axes)
        label_count = global_sums[0]
        loss_value = global_sums[1] / label_count
        g_two = ((jnp.exp(log_probs) - one_hot) * (weights / label_count)[:, None]).astype(jnp.bfloat16)
        dy_two = collect(g_two).astype(jnp.bfloat16)
        dw_two = lax.psum(lax.dot_general(h_one, dy_two, (((0,), (0,)), ((), ())), preferred_element_type=jnp.float32), all_axes)
        dh_one = lax.dot_general(dy_two, w_two_lo, (((1,), (1,)), ((), ())), preferred_element_type=jnp.float32)
        g_one = jnp.where(z_one > 0.0, dh_one, 0.0).astype(jnp.bfloat16)
        dy_one = collect(g_one).astype(jnp.bfloat16)
        dw_one = lax.psum(lax.dot_general(feat_blk, dy_one, (((0,), (0,)), ((), ())), preferred_element_type=jnp.float32), all_axes)
        return loss_value, dw_one, dw_two

    return jax.shard_map(device_step, mesh=mesh, in_specs=(P(None, "nodes", "rep"), row_spec, P(), P(), row_spec, row_spec), out_specs=(P(), P(), P()), check_vma=False)
```

profile of v0, /device:TPU:1, one launch (start us, length us, event | category | flops | bytes accessed | tf_op | source)
XLA Modules:
  0.0 577.7 jit_solution(14816284508689358921)
XLA Ops:
  7.2 0.0 copy-start
  7.2 0.0 reduce-scatter.17.cloned.1.call-start
  7.2 0.7 copy-done
  8.0 1.1 convolution_convert_fusion
  9.0 15.1 %all_gather.16 = bf16[1536,256]{1,0:T(8,128)(2,1)S(1)} all-gather(bf16[192,256]{1,0:T(8,128)(2,1)S(1)} %convolution_convert_fusion), channel_id=1, replica_groups=mesh['rep'=16,'nodes'=8] {'nodes'}, dimensions={0}, use_global_device_ids=true | all-gather | bytes 884736 | tf_op jit(solution)/shard_map/all_gather | solution.py:17
  24.1 0.0 copy-start.2
  24.1 8.0 %convolution_bitcast_fusion.2 = f32[16,192,256]{2,1,0:T(8,128)} fusion(bf16[16,192,1536]{2,1,0:T(8,128)(2,1)} %param.6, bf16[1536,256]{1,0:T(8,128)(2,1)S(1)} %all_gather.16), kind=kOutput, calls=%fused_computation.2 | convolution fusion | flops 2415919104 | bytes 13369344 | tf_op jit(solution)/shard_map/dot_general | solution.py:18
  32.1 0.0 copy-start.3
  32.1 0.0 copy-start.4
  32.1 0.0 reduce-scatter.17.cloned.1.call-update
  32.1 0.0 reduce-scatter.19.cloned.1.call-start
  32.2 76.2 %reduce-scatter.17.cloned.1.call-done = f32[1,192,256]{2,1,0:T(8,128)} async-done(((f32[16,192,256]{2,1,0:T(8,128)}), f32[1,192,256]{2,1,0:T(8,128)}) %reduce-scatter.17.cloned.1.call-update) | async-done | bytes 196624
  108.4 0.0 copy-done.2
  108.4 1.1 fusion.1
  109.4 15.3 %all-gather.1 = bf16[8,192,40]{1,2,0:T(8,128)(2,1)S(1)} all-gather(bf16[1,192,40]{1,2,0:T(8,128)(2,1)S(1)} %fusion.1), channel_id=1, replica_groups=mesh['rep'=16,'nodes'=8] {'nodes'}, dimensions={0}, use_global_device_ids=true | all-gather | bytes 138240 | tf_op jit(solution)/shard_map/all_gather | solution.py:17
  124.8 0.2 reshape.67
  125.0 7.5 %convolution_bitcast_fusion.3 = f32[16,192,40]{1,2,0:T(8,128)} fusion(bf16[1536,40,1]{0,1,2:T(8,128)(2,1)S(1)} %reshape.67, bf16[16,192,1536]{2,1,0:T(8,128)(2,1)} %param.6), kind=kOutput, calls=%fused_computation.3 | convolution fusion | flops 377487360 | bytes 10051584 | tf_op jit(solution)/shard_map/dot_general | solution.py:18
  132.4 0.0 copy-start.1
  132.4 0.0 reduce-scatter.19.cloned.1.call-update
  132.5 0.0 reduce-scatter.13.cloned.1.call-start
  132.5 70.2 %reduce-scatter.19.cloned.1.call-done = f32[1,192,40]{1,2,0:T(8,128)} async-done(((f32[16,192,40]{1,2,0:T(8,128)}), f32[1,192,40]{1,2,0:T(8,128)}) %reduce-scatter.19.cloned.1.call-update) | async-done | bytes 30736
  202.7 0.8 reduce_max.10
  203.5 0.8 exponential_reduce_fusion
  204.3 0.0 copy-done.3
  204.4 0.8 select_reduce_fusion
  205.2 0.0 copy-done.4
  205.2 0.6 convert_reduce_fusion
  206.4 0.7 pad_maximum_fusion
  207.1 65.8 %psum.21 = f32[2]{0:T(128)S(1)} all-reduce(f32[2]{0:T(128)S(1)} %pad_maximum_fusion), channel_id=1, replica_groups=mesh['rep'=16,'nodes'=8] {'rep','nodes'}, use_global_device_ids=true, to_apply=%region_7.8 | all-reduce | flops 2 | bytes 16 | tf_op jit(solution)/shard_map/psum | solution.py:35
  273.0 0.6 fusion.15
  273.6 0.6 convert_divide_fusion
  274.2 0.8 multiply_convert_fusion
  275.0 16.4 %all_gather.18 = bf16[16,192,40]{1,2,0:T(8,128)(2,1)S(1)} all-gather(bf16[1,192,40]{1,2,0:T(8,128)(2,1)S(1)} %multiply_convert_fusion), channel_id=1, replica_groups=mesh['rep'=16,'nodes'=8] {'rep'}, dimensions={0}, use_global_device_ids=true | all-gather | bytes 261120 | tf_op jit(solution)/shard_map/all_gather | solution.py:22
  291.5 5.4 convolution_bitcast_fusion.1
  296.9 1.2 copy.14
  298.0 0.0 reduce-scatter.13.cloned.1.call-update
  298.0 0.0 all-gather.4.cloned.1.call-start
  298.1 32.1 %reduce-scatter.13.cloned.1.call-done = f32[192,40]{1,0:T(8,128)} async-done(((f32[1536,40]{1,0:T(8,128)}), f32[192,40]{1,0:T(8,128)}) %reduce-scatter.13.cloned.1.call-update) | async-done | bytes 30736
  330.2 1.0 copy.15
  331.2 0.0 copy-done.1
  331.2 0.8 fusion
  332.0 0.0 all-gather.4.cloned.1.call-update
  332.1 0.0 reduce-scatter.15.cloned.1.call-start
  332.1 43.9 %all-gather.4.cloned.1.call-done = bf16[3072,256]{1,0:T(8,128)(2,1)} async-done(((bf16[192,256]{1,0:T(8,128)(2,1)}), bf16[3072,256]{1,0:T(8,128)(2,1)}) %all-gather.4.cloned.1.call-update) | async-done | bytes 1572880 | tf_op jit(solution)/shard_map/all_gather | solution.py:22
  376.0 5.7 convolution_bitcast_fusion
  381.8 1.6 copy.16
  383.4 0.0 reduce-scatter.15.cloned.1.call-update
  383.4 0.0 all-reduce.4.cloned.1.call-start
  384.8 30.5 %reduce-scatter.15.cloned.1.call-done = f32[192,256]{1,0:T(8,128)} async-done(((f32[1536,256]{1,0:T(8,128)}), f32[192,256]{1,0:T(8,128)}) %reduce-scatter.15.cloned.1.call-update) | async-done | bytes 196624
  415.3 1.0 copy.17
  416.3 0.8 convolution_bitcast_fusion.4
  417.1 0.0 all-reduce.4.cloned.1.call-update
  417.2 0.1 fusion.6
  417.3 67.8 %psum.23 = f32[256,40]{0,1:T(8,128)} all-reduce(f32[256,40]{0,1:T(8,128)S(1)} %fusion.6), channel_id=1, replica_groups=mesh['rep'=16,'nodes'=8] {'rep','nodes'}, use_global_device_ids=true, to_apply=%region_11.12 | all-reduce | flops 10240 | bytes 81920 | tf_op jit(solution)/shard_map/psum | solution.py:40
  485.1 83.0 %all-reduce.4.cloned.1.call-done = f32[128,256]{0,1:T(8,128)} async-done(((f32[128,256]{0,1:T(8,128)}), f32[128,256]{0,1:T(8,128)}) %all-reduce.4.cloned.1.call-update) | async-done | bytes 131088 | tf_op jit(solution)/shard_map/psum | solution.py:44
  568.1 1.7 copy.13
  (2 shorter events, 0.0 us)
Async XLA Ops:
  7.2 0.8 copy-start
  7.2 101.2 %reduce-scatter.17.cloned.1.call-start = ((), (), s32[]{:S(2)}) async-start(), calls=%async_computation.8 | async-start | bytes 3342336
  24.1 84.3 %copy-start.2 = (f32[256,40]{0,1:T(8,128)S(1)}, f32[256,40]{0,1:T(8,128)}, u32[]{:S(2)}) copy-start(f32[256,40]{0,1:T(8,128)} %param.9) | copy-start | bytes 122884
  32.1 172.3 %copy-start.3 = (s32[192]{0:T(256)S(1)}, s32[192]{0:T(256)}, u32[]{:S(2)}) copy-start(s32[192]{0:T(256)} %param.10) | copy-start | bytes 2308
  32.1 173.1 %copy-start.4 = (s32[192]{0:T(256)S(1)}, s32[192]{0:T(256)}, u32[]{:S(2)}) copy-start(s32[192]{0:T(256)} %param.11) | copy-start | bytes 2308
  32.1 170.6 %reduce-scatter.19.cloned.1.call-start = ((), (), s32[]{:S(2)}) async-start(), calls=%async_computation.9 | async-start | bytes 696320
  132.4 198.7 %copy-start.1 = (f32[1,192,256]{2,1,0:T(8,128)S(1)}, f32[1,192,256]{2,1,0:T(8,128)}, u32[]{:S(2)}) copy-start(f32[1,192,256]{2,1,0:T(8,128)} %reduce-scatter.17.cloned.1.call-done) | copy-start | bytes 589828
  132.5 197.7 %reduce-scatter.13.cloned.1.call-start = ((), (), s32[]{:S(2)}) async-start(), calls=%async_computation.6 | async-start | bytes 884736
  298.0 78.0 %all-gather.4.cloned.1.call-start = ((), (), s32[]{:S(2)}) async-start(), calls=%async_computation.5 | async-start | bytes 1671168 | tf_op jit(solution)/shard_map/all_gather | solution.py:22
  332.1 83.2 %reduce-scatter.15.cloned.1.call-start = ((), (), s32[]{:S(2)}) async-start(), calls=%async_computation.7 | async-start | bytes 1769472
  383.4 184.7 %all-reduce.4.cloned.1.call-start = ((), (), s32[]{:S(2)}) async-start(), calls=%async_computation.4 | async-start | bytes 262144 | tf_op jit(solution)/shard_map/psum | solution.py:44
Sparse Core Ops, SparseCore 0:
  32.2 76.0 reduce-scatter.16
  132.6 70.1 reduce-scatter.18
  298.2 31.9 reduce-scatter.12
  332.8 43.2 all-gather.3
  383.5 31.6 reduce-scatter.14
  420.4 147.6 all-reduce.3
where the time goes:
time: 579 us; the launch traced here: 578 us
  waiting for transfers between devices  336 us (58%)
  blocking collectives  180 us (31%)
  matrix products  30.5 us (5%)
  between operations  17.3 us (3%)
  local copies, waits for them, and re-layouts  7.98 us (1%)
    unnamed x10, waiting for transfers between devices  209 us
    psum x1, waiting for transfers between devices, device_step(): lax.psum(lax.dot_general(feat_blk, dy_one, (((0,), (0,)), ((), ())), pref...  83 us
    psum x1, blocking collectives, device_step(): lax.psum(lax.dot_general(h_one, dy_two, (((0,), (0,)), ((), ())), preferr...  67.8 us
    psum x1, blocking collectives, device_step(): global_sums = lax.psum(local_sums, all_axes)  65.8 us
    all_gather x1, waiting for transfers between devices, collect(): gathered = lax.all_gather(g_blk, 'rep', axis=0)  43.9 us
    all_gather x2, blocking collectives, spread(): gathered = lax.all_gather(y_blk, 'nodes', axis=0, tiled=True)  30.4 us
    all_gather x1, blocking collectives, collect(): gathered = lax.all_gather(g_blk, 'rep', axis=0)  16.4 us
    dot_general x2, matrix products, spread(): lax.dot_general(adj_blk, gathered, (((2,), (0,)), ((), ())), preferred_el...  15.4 us
  transfers between devices with their start and end apart: 6, of which 6 were waited for; matrix products, arithmetic and copies ran while one was open for 0% of the time, Pallas kernels for 0%

commit v1 on v0

v1 whole, which is shorter than its diff:
```python
import jax
import jax.numpy as jnp
from jax import lax
from jax.experimental import pallas as pl
from jax.experimental.pallas import tpu as pltpu
from jax.sharding import PartitionSpec as P

MESH = pl.DeviceIdType.MESH
F32, BF16 = jnp.float32, jnp.bfloat16
T, G, N = 2, 4, 8
LANE, HID, CLS, ROW = 128, 256, 40, 192
PK = ROW // 3
TALL, WIDE = 16 * ROW, N * ROW
PAIR = T * ROW
N_SEM = 320


def ring(v, k):
    return (v + k + G) % G


def dot(a, b, ca, cb):
    return lax.dot_general(a, b, (((ca,), (cb,)), ((), ())), preferred_element_type=F32)


def span(start, size):
    return pl.ds(start if isinstance(start, int) else pl.multiple_of(start, size), size)


class Net:
    def __init__(self, send_sem, recv_sem):
        rep, node = lax.axis_index("rep"), lax.axis_index("nodes")
        self.z, self.y, self.x, self.c = rep // G, rep % G, node // T, node % T
        self.sems, self.used, self.ends = (send_sem, recv_sem), 0, []

    def dev(self, **place):
        z, y, x, c = (place.get(k, getattr(self, k)) for k in "zyxc")
        return (z * G + y, x * T + c)

    def near(self, axis, k):
        return self.dev(**{axis: ring(getattr(self, axis), k)})

    def partner(self):
        return self.dev(c=1 - self.c)

    def copy(self, src, dst, device, k):
        send, recv = (sem.at[k] for sem in self.sems)
        return pltpu.make_async_remote_copy(src_ref=src, dst_ref=dst, send_sem=send, recv_sem=recv, device_id=device, device_id_type=MESH)

    def send(self, src, dst, device):
        copy = self.copy(src, dst, device, self.used)
        self.used += 1
        copy.start()
        self.ends.append(copy.wait_send)
        return copy

    def rep_all(self, src, dst, before=None):
        base, self.used = self.used, self.used + G * G

        def place(j, sign):
            k = (j * 5) % (G * G)
            return ring(self.z, sign * (k // G)), ring(self.y, sign * (k % G)), base + k

        def start(j, _):
            z, y, k = place(j, 1)
            if before is not None:
                before(z, y)
            self.copy(src(z, y), dst, self.dev(z=z, y=y), k).start()
            return _

        def each(fn):
            def body(j, _):
                z, y, k = place(j, -1)
                self.copy(dst, dst, self.dev(z=z, y=y), k).wait_recv()
                fn(z, y)
                return _
            lax.fori_loop(1, G * G, body, 0)

        def end(j, _):
            z, y, k = place(j, 1)
            self.copy(dst, dst, self.dev(z=z, y=y), k).wait_send()
            return _

        lax.fori_loop(1, G * G, start, 0)
        self.ends.append(lambda: lax.fori_loop(1, G * G, end, 0))
        return each

    def peers(self):
        out = [self.partner()]
        for k in (1, 2, 3):
            out += [self.near(axis, k) for axis in "xyz"]
            out.append(self.dev(x=ring(self.x, k), c=1 - self.c))
        return out


class Tree:
    def __init__(self, net, axis, at, far, near):
        self.net, self.at, self.far, self.near = net, at, far, near
        self.p = getattr(net, axis)
        self.side = net.near(axis, 1), net.near(axis, -1)

    def start(self):
        self.first = [self.net.send(self.at(ring(self.p, T), d), self.far(d), self.side[d]) for d in (0, 1)]
        self.arrive = []

    def free(self, d):
        t = ring(self.p, 1 - T * d)
        self.arrive.append(self.net.send(self.at(t, 1 - d), self.near(d, 1 - d), self.side[d]))

    def relay(self):
        for d in (0, 1):
            self.first[d].wait_recv()
            mine = self.at(ring(self.p, 1 - T * d), d)
            mine[...] = mine[...] + self.far(d)[...]
            self.arrive.append(self.net.send(mine, self.near(d, d), self.side[d]))

    def end(self):
        for copy in self.arrive:
            copy.wait_recv()


class RepSum:
    def __init__(self, net, terms, far, near, mid, last):
        self.net, self.terms, self.near, self.mid, self.last = net, terms, near, mid, last
        self.size = near.shape[-T]
        q = self.size // T
        self.parts = [(h, s) for s in (0, 1) for h in (0, 1)]
        self.tree = {}
        for h, s in self.parts:

            def at(t, d, h=h, s=s):
                row = pl.ds((h * T + s) * self.size + d * q, q)
                return terms.at[t, :, row] if h else terms.at[:, t, row]

            self.tree[h, s] = Tree(
                net, "yz"[h], at, lambda d, h=h, s=s: far.at[h, s, d], lambda d, e, h=h, s=s: near.at[h, s, d, :, pl.ds(e * q, q)]
            )

    def start(self, h):
        for s in (0, 1):
            self.tree[h, s].start()

    def free(self, h):
        for s in (0, 1):
            for d in (0, 1):
                self.tree[h, s].free(d)

    def finish(self, out):
        net, size = self.net, self.size
        for part in self.parts:
            self.tree[part].relay()
        arrivals = []
        for h, s in self.parts:
            tree, mid = self.tree[h, s], self.mid.at[h, s]
            tree.end()
            row = pl.ds((h * T + s) * size, size)
            own = self.terms[tree.p, :, row] if h else self.terms[:, tree.p, row]
            mid[...] = own + self.near[h, s, 0] + self.near[h, s, 1]
            axis = "zy"[h]
            arrivals.append(exchange(net, axis, lambda t: mid.at[t], self.last.at[h, s]))
        for (h, s), copies in zip(self.parts, arrivals):
            for copy in copies:
                copy.wait_recv()
            p = net.y if h else net.z
            total = self.mid[h, s, p]
            for k in (1, 2, 3):
                total = total + self.last[h, s, ring(p, k)]
            out[pl.ds((h * T + s) * size, size)] = total


def exchange(net, axis, src, buf):
    p = getattr(net, axis)
    return [net.send(src(ring(p, k)), buf.at[p], net.near(axis, k)) for k in (2, 1, 3)]


def gather_nodes(net, buf):
    mine = buf.at[net.x * T + net.c]
    out = []
    for k in (2, 1, 3):
        out.append(net.send(mine, mine, net.near("x", k)))
        out.append(net.send(mine, mine, net.dev(x=ring(net.x, k), c=1 - net.c)))
    return out + [net.send(mine, mine, net.partner())]


def gather_pairs(net, buf):
    block = lambda k: buf.at[ring(net.x, k) * T + net.c]
    own = block(0)
    over = [net.send(own, own, net.partner())]
    come = [(k, net.send(own, own, net.near("x", k))) for k in (1, 3, 2)]
    for k, copy in come:
        copy.wait_recv()
        over.append(net.send(block(-k), block(-k), net.partner()))
    for copy in over:
        copy.wait_recv()


def gather_rep(net, buf):
    q = buf.shape[T] // G

    def move(s, u, v, device, part=None):
        h = s["h"]
        row = pl.ds(h * T * q, T * q) if part is None else pl.ds((h * T + part) * q, q)
        ref = buf.at[u, v, row] if h else buf.at[v, u, row]
        return net.send(ref, ref, device)

    state = []
    for h in (0, 1):
        first, second = ("y", "z") if h == 0 else ("z", "y")
        p, v = getattr(net, first), getattr(net, second)
        s = dict(h=h, p=p, v=v, up=net.near(second, 1), down=net.near(second, -1), over=[])
        s["near"] = [(k, move(s, p, v, net.near(first, k))) for k in (1, 3)]
        s["near"].append((T, move(s, p, v, net.near(first, T))))
        state.append(s)

    def cross(s, k):
        u = ring(s["p"], k)
        s["over"].append((u, move(s, u, s["v"], s["up"]), move(s, u, s["v"], s["down"])))

    for s in state:
        cross(s, 0)
    for n in range(3):
        for s in state:
            k, copy = s["near"][n]
            copy.wait_recv()
            cross(s, -k)
    last = []
    for n in range(G):
        for s in state:
            u, up, down = s["over"][n]
            up.wait_recv()
            last.append(move(s, u, ring(s["v"], -1), s["up"], 0))
            down.wait_recv()
            last.append(move(s, u, ring(s["v"], 1), s["down"], 1))
    for copy in last:
        copy.wait_recv()


def lanes(shape):
    return lax.broadcasted_iota(jnp.int32, shape, len(shape) - 1)


def pack(v):
    return v[:PK] + pltpu.roll(v[PK : T * PK], CLS, 1) + pltpu.roll(v[T * PK :], T * CLS, 1)


def unpack(v):
    keep = lanes((PK, LANE)) < CLS
    parts = [v, pltpu.roll(v, LANE - CLS, 1), pltpu.roll(v, LANE - T * CLS, 1)]
    return [jnp.where(keep, part, 0.0) for part in parts]


def scratch_shapes():
    half, piece = HID // T, ROW // G
    return dict(
        a_v=((TALL, WIDE), BF16),
        xg=((N, ROW, LANE), BF16),
        cg=((N, N, LANE), F32),
        y1=((WIDE, HID), BF16),
        zp=((G, G, ROW, HID), F32),
        far=((T, T, T, G, piece // T, HID), F32),
        near=((T, T, T, G, piece, HID), F32),
        mid=((T, T, G, piece, HID), F32),
        last=((T, T, G, piece, HID), F32),
        z1=((ROW, HID), F32),
        h1=((ROW, HID), BF16),
        w2p=((LANE, HID), F32),
        y2g=((N, PK, LANE), BF16),
        y2u=((WIDE, LANE), BF16),
        zq=((G, G, PK, LANE), F32),
        zi=((G, G, PK, LANE), F32),
        g2g=((G, G, PK, LANE), BF16),
        g2u=((TALL, LANE), BF16),
        d2=((G, piece, PAIR), F32),
        d2i=((G, piece, PAIR), F32),
        d2s=((T, piece, PAIR), F32),
        d2t=((PAIR, LANE), F32),
        g1g=((G, G, ROW, HID), BF16),
        e1=((G, HID, PAIR), F32),
        e1o=((G, half, PAIR), F32),
        e1s=((G, half, PAIR), F32),
        e1far=((T, half // T, PAIR), F32),
        e1near=((T, half, PAIR), F32),
        w2s=((T, piece, LANE), F32),
        w2o=((piece, LANE), F32),
        ra=((G, G, G * G, LANE), F32),
        rai=((G, G, G * G, LANE), F32),
        rx=((G, G * G, LANE), F32),
        rf=((T, G, G, G * G, LANE), F32),
    )


def kernel(adj, x_ref, w1_ref, w2_ref, lab_ref, msk_ref, out_ref, *scratch):
    names = list(scratch_shapes())
    s = dict(zip(names, scratch))
    send_sem, recv_sem, load_sem = scratch[len(names) :]
    net = Net(send_sem, recv_sem)
    z, y, x, c = net.z, net.y, net.x, net.c
    a_v = s["a_v"]

    tall = [pl.ds(k * (TALL // G), TALL // G) for k in range(G)]
    loads = [pltpu.make_async_copy(adj.at[rows], a_v.at[rows], load_sem.at[k]) for k, rows in enumerate(tall)]
    for load in loads:
        load.start()

    barrier = pltpu.get_barrier_semaphore()
    peers = net.peers()
    for peer in peers:
        pl.semaphore_signal(barrier, inc=1, device_id=peer, device_id_type=MESH)

    me = x * T + c
    xg, cg = s["xg"], s["cg"]
    xg[me] = x_ref[...]
    mask_row = msk_ref[...].astype(F32).reshape(1, ROW)
    label_row = lab_ref[...].reshape(1, ROW)
    cg[me] = jnp.broadcast_to(jnp.sum(mask_row, axis=1, keepdims=True), (N, LANE))
    w2p = s["w2p"]
    w2p[...] = jnp.zeros((LANE, HID), F32)
    w2p[:CLS] = w2_ref[...]
    w2b = w2p[...].astype(BF16)
    w1b = w1_ref[...].astype(BF16)

    pl.semaphore_wait(barrier, len(peers))

    counts = gather_nodes(net, cg)
    gather_pairs(net, xg)
    y1 = s["y1"]
    y1[...] = dot(xg[...].reshape(WIDE, LANE), w1b, 1, 0).astype(BF16)
    for load in loads:
        load.wait()

    zp = s["zp"]

    def block(zz, yy):
        return a_v[span((zz * G + yy) * ROW, ROW)]

    def z1_loop(count, place):
        def body(k, _):
            zz, yy = place(k)
            zp[zz, yy] = dot(block(zz, yy), y1[...], 1, 0)
            return _
        lax.fori_loop(0, count, body, 0)

    sum1 = RepSum(net, zp, s["far"], s["near"], s["mid"], s["last"])
    z1_loop(G, lambda k: (k, ring(y, 2)))
    sum1.start(0)
    z1_loop(3, lambda k: (ring(z, 2), ring(y, k - 1)))
    sum1.start(1)
    z1_loop(6, lambda k: (ring(z, k // 2 - 1), ring(y, 1 + 2 * (k % 2))))
    sum1.free(0)
    z1_loop(3, lambda k: (ring(z, k - 1), y))
    sum1.free(1)
    z1 = s["z1"]
    sum1.finish(z1)

    h1 = s["h1"]
    h1[...] = jnp.maximum(z1[...], 0.0).astype(BF16)
    y2 = dot(h1[...], w2b, 1, 1).astype(BF16).astype(F32)
    y2g, y2u = s["y2g"], s["y2u"]
    y2g[me] = pack(y2).astype(BF16)
    for copy in counts + gather_nodes(net, y2g):
        copy.wait_recv()

    def spread(src, dst, base):
        for g, part in enumerate(unpack(src.astype(F32))):
            dst[span(base * ROW + g * PK, PK)] = part.astype(BF16)

    def spread_y2(j, _):
        spread(y2g[j], y2u, j)
        return _

    lax.fori_loop(0, N, spread_y2, 0)

    zq, zi = s["zq"], s["zi"]
    count = jnp.sum(cg[...], axis=0)[:1]
    at_count = lanes((PK, LANE)) == 3 * CLS
    count = jnp.where(at_count, jnp.broadcast_to(count, (PK, LANE)), 0.0)

    def z2_block(zz, yy):
        zq[zz, yy] = pack(dot(block(zz, yy), y2u[...], 1, 0)) + count

    arrivals = net.rep_all(lambda zz, yy: zq.at[zz, yy], zi.at[z, y], z2_block)
    z2_block(z, y)
    zi[z, y] = zq[z, y]
    mask_all = jnp.broadcast_to(mask_row, (LANE, ROW)).T
    classes = lax.broadcasted_iota(jnp.int32, (LANE, ROW), 0)
    one_hot = (jnp.broadcast_to(label_row, (LANE, ROW)) == classes).astype(F32).T
    arrivals(lambda zz, yy: None)
    packed = jnp.sum(zi[...].reshape(G * G, PK, LANE), axis=0)

    total = jnp.sum(jnp.where(at_count, packed, 0.0), axis=1, keepdims=True)
    total = jnp.concatenate([total, total, total], axis=0)
    logits = jnp.concatenate(unpack(packed), axis=0)
    valid = lanes((ROW, LANE)) < CLS
    top = jnp.max(jnp.where(valid, logits, -jnp.inf), axis=1, keepdims=True)
    shifted = jnp.where(valid, logits - top, 0.0)
    norm = jnp.sum(jnp.where(valid, jnp.exp(shifted), 0.0), axis=1, keepdims=True)
    log_probs = shifted - jnp.log(norm)
    picked = jnp.where(valid, -(mask_all * (one_hot * log_probs)), 0.0)
    loss_part = jnp.sum(picked, axis=0, keepdims=True)
    g2 = jnp.where(valid, (jnp.exp(log_probs) - one_hot) * (mask_all / total), 0.0).astype(BF16).astype(F32)
    g2g, g2u = s["g2g"], s["g2u"]
    g2g[z, y] = pack(g2).astype(BF16)

    def spread_g2(zz, yy):
        spread(g2g[zz, yy], g2u, zz * G + yy)

    arrivals = net.rep_all(lambda zz, yy: g2g.at[z, y], g2g.at[z, y])
    spread_g2(z, y)
    arrivals(spread_g2)

    d2, d2i, d2s, d2t = (s[k] for k in ("d2", "d2i", "d2s", "d2t"))
    rows = d2.shape[1]

    def d2_block(k, _):
        part = dot(g2u[...], a_v[:, span(k * T * PAIR, T * PAIR)], 0, 0)
        d2[T * k] = part[:rows, :PAIR]
        d2[T * k + 1] = part[:rows, PAIR:]
        return _

    lax.fori_loop(0, T, d2_block, 0)
    for copy in exchange(net, "x", lambda t: d2.at[t], d2i):
        copy.wait_recv()
    d2i[x] = d2[x]
    d2s[c] = jnp.sum(d2i[...], axis=0)
    net.send(d2s.at[c], d2s.at[c], net.partner()).wait_recv()
    d2t[...] = jnp.concatenate([d2s[0] + d2s[1], jnp.zeros((LANE - rows, PAIR), F32)], axis=0).T
    dy2 = d2t[span(c * ROW, ROW)].astype(BF16)

    dh1 = dot(dy2, w2b, 1, 0)
    g1g = s["g1g"]
    g1g[z, y] = jnp.where(z1[...] > 0.0, dh1, 0.0).astype(BF16)

    dw2_t = dot(dy2, h1[...], 0, 0)[:CLS]
    loss_tile = jnp.concatenate([loss_part, jnp.zeros((N - 1, LANE), F32)], axis=0)
    w2s, w2o = s["w2s"], s["w2o"]
    for h in (0, 1):
        w2s[h, :CLS] = dw2_t[:, h * LANE : (h + 1) * LANE]
        w2s[h, CLS:] = loss_tile
    swap = net.send(w2s.at[1 - c], w2o, net.partner())

    gather_rep(net, g1g)
    swap.wait_recv()

    e1, e1o, e1s, e1far, e1near = (s[k] for k in ("e1", "e1o", "e1s", "e1far", "e1near"))
    half = HID // T
    q = half // T
    part = lambda d: pl.ds(d * q, q)
    tree = Tree(net, "x", lambda t, d: e1s.at[t, part(d)], lambda d: e1far.at[d], lambda d, e: e1near.at[d, part(e)])

    def e1_block(k):
        t = ring(x, k)
        e1[t] = dot(g1g[...].reshape(TALL, HID), a_v[:, span(t * PAIR, PAIR)], 0, 0)
        return t, net.send(e1.at[t, span((1 - c) * half, half)], e1o.at[t], net.partner())

    def e1_join(t, copy):
        copy.wait_recv()
        e1s[t] = e1[t, span(c * half, half)] + e1o[t]

    opposite = e1_block(2)
    right = e1_block(1)
    e1_join(*opposite)
    tree.start()
    left = e1_block(3)
    e1_join(*right)
    tree.free(0)
    own = e1_block(0)
    e1_join(*left)
    tree.free(1)
    tree.relay()
    e1_join(*own)
    tree.end()
    dy1 = (e1s[x] + e1near[0] + e1near[1]).astype(BF16)
    dw1_t = dot(dy1, xg[pl.ds(x * T, T)].reshape(PAIR, LANE), 1, 0)

    ra, rai, rx, rf = (s[k] for k in ("ra", "rai", "rx", "rf"))
    tile = G * G
    ra[:T] = dw1_t.reshape(T, G, tile, LANE)
    ra[T, :3] = (w2s[c] + w2o[...]).reshape(3, tile, LANE)
    ra[T, 3] = jnp.zeros((tile, LANE), F32)
    ra[3] = jnp.zeros((G, tile, LANE), F32)
    arrivals = net.rep_all(lambda zz, yy: ra.at[zz, yy], rai.at[z, y])
    rai[z, y] = ra[z, y]
    arrivals(lambda zz, yy: None)
    rx[x] = jnp.sum(rai[...].reshape(tile, tile, LANE), axis=0)
    for copy in exchange(net, "x", lambda t: rx.at[x], rx):
        copy.wait_recv()
    rf[c, z, y] = jnp.sum(rx[...], axis=0)
    arrivals = net.rep_all(lambda zz, yy: rf.at[c, z, y], rf.at[c, z, y])
    arrivals(lambda zz, yy: None)
    net.send(rf.at[c], rf.at[c], net.partner()).wait_recv()

    out_ref[...] = rf[:, :3].reshape(T, 3 * G * tile, LANE)
    out_ref[0, span(3 * G * tile - N, N)] = jnp.broadcast_to(total[:1], (N, LANE))
    for end in net.ends:
        end()


def unpack_kernel(sums, loss_ref, dw1_ref, dw2_ref):
    for h in (0, 1):
        half = span(h * LANE, LANE)
        dw1_ref[:, half] = sums[h, :LANE].T
        dw2_ref[:, half] = sums[h, LANE : LANE + CLS]
    loss = jnp.sum(sums[0, LANE + CLS : LANE + CLS + N])
    loss_ref[0, 0] = loss / jnp.max(sums[0, sums.shape[1] - N :])


def solution(mesh):
    vmem, smem = pl.BlockSpec(memory_space=pltpu.VMEM), pl.BlockSpec(memory_space=pltpu.SMEM)
    struct = lambda *shape: jax.ShapeDtypeStruct(shape, F32)

    def device_step(adj_blk, feat_blk, w_one, w_two, label_blk, mask_blk):
        sems = [pltpu.SemaphoreType.DMA((n,)) for n in (N_SEM, N_SEM, G)]
        sums = pl.pallas_call(
            kernel,
            out_shape=struct(T, 3 * G * G * G, LANE),
            in_specs=[pl.BlockSpec(memory_space=pl.ANY)] + [vmem] * 5,
            out_specs=vmem,
            scratch_shapes=[pltpu.VMEM(shape, dtype) for shape, dtype in scratch_shapes().values()] + sems,
            compiler_params=pltpu.CompilerParams(collective_id=0, has_side_effects=True, vmem_limit_bytes=56 << 20),
        )(adj_blk.reshape(TALL, WIDE), feat_blk, w_one, w_two.T, label_blk, mask_blk)
        loss, dw1, dw2 = pl.pallas_call(
            unpack_kernel,
            out_shape=(struct(1, 1), struct(LANE, HID), struct(CLS, HID)),
            in_specs=[vmem],
            out_specs=(smem, vmem, vmem),
        )(sums)
        return loss.reshape(()), dw1, dw2.T

    row_spec = P(("rep", "nodes"))
    return jax.shard_map(
        device_step,
        mesh=mesh,
        in_specs=(P(None, "nodes", "rep"), row_spec, P(), P(), row_spec, row_spec),
        out_specs=(P(), P(), P()),
        check_vma=False,
    )
```

time: 579 us -> 115 us (0.20)
  waiting for transfers between devices: 336 us -> 0 us
  blocking collectives: 180 us -> 0 us
  Pallas kernels: 0 us -> 114 us
  matrix products: 30.5 us -> 0 us
  between operations: 17.3 us -> 0.64 us
  local copies, waits for them, and re-layouts: 7.98 us -> 0 us
    unnamed x10 -> x0, waiting for transfers between devices: 209 us -> none
    psum x2 -> x0, blocking collectives: 134 us -> none  [the longest x1 67.8 us: device_step(): lax.psum(lax.dot_general(h_one, dy_two, (((0,), (0,)), ((), ())), preferr...]
    pallas_call x0 -> x2, Pallas kernels: none -> 114 us  [the longest x1 112 us: device_step(): pl.pallas_call(kernel, out_shape=struct(T, 3 * G * G * G, LANE), in_specs...]
    psum x1 -> x0, waiting for transfers between devices: 83 us -> none  [device_step(): lax.psum(lax.dot_general(feat_blk, dy_one, (((0,), (0,)), ((), ())), pref...]
    all_gather x3 -> x0, blocking collectives: 46.9 us -> none  [the longest x2 30.4 us: spread(): gathered = lax.all_gather(y_blk, 'nodes', axis=0, tiled=True)]
    all_gather x1 -> x0, waiting for transfers between devices: 43.9 us -> none  [collect(): gathered = lax.all_gather(g_blk, 'rep', axis=0)]
    dot_general x9 -> x0, matrix products: 30.5 us -> none  [the longest x2 15.4 us: spread(): lax.dot_general(adj_blk, gathered, (((2,), (0,)), ((), ())), preferred_el...]
    unnamed x16 -> x0, local copies, waits for them, and re-layouts: 7.36 us -> none
  transfers between devices with their start and end apart: 6 -> 0, of which waited for: 6 -> 0; matrix products, arithmetic and copies ran while one was open for 0% -> 0% of each run, Pallas kernels for 0% -> 0%
where the time goes in v1:
time: 115 us
  Pallas kernels  114 us (99%)
    pallas_call x1, Pallas kernels, device_step(): pl.pallas_call(kernel, out_shape=struct(T, 3 * G * G * G, LANE), in_specs...  112 us

profile of v1, /device:TPU:1, one launch (start us, length us, event | category | flops | bytes accessed | tf_op | source)
XLA Modules:
  0.0 114.5 jit_solution(13696013587359409513)
XLA Ops:
  0.6 112.2 %shard_map.85.sums = f32[2,192,128]{2,1,0:T(8,128)} custom-call(bf16[3072,1536]{1,0:T(8,128)(2,1)} %bitcast.4, bf16[192,128]{1,0:T(8,128)(2,1)} %x_ref.1, f32[128,256]{1,0:T(8,128)} %w1_ref.1, f32[40,256]{1,0:T(8,128)} %bitcast.5, s32[192]{0:T(256)} %lab_ref.1, s32[192]{0:T(256)} %msk_ref.1), custom_call_target="tpu_custom_call" | custom-call | tf_op jit(solution)/shard_map/pallas_call | solution.py:513
  112.8 1.7 %shard_map.86 = (f32[1,1]{1,0:T(1,128)}, f32[128,256]{1,0:T(8,128)}, f32[40,256]{1,0:T(8,128)}) custom-call(f32[2,192,128]{2,1,0:T(8,128)} %shard_map.85.sums), custom_call_target="tpu_custom_call" | custom-call | tf_op jit(solution)/shard_map/pallas_call | solution.py:521

commit v2 on v1

--- a/solution.py
+++ b/solution.py
@@ -54,35 +54,37 @@
         self.ends.append(copy.wait_send)
         return copy
 
-    def rep_all(self, src, dst, before=None):
+    def rep_all(self, src, dst, before=None, flip=False):
         base, self.used = self.used, self.used + G * G
+        count = G * G if flip else G * G - 1
+        core = 1 - self.c if flip else self.c
 
         def place(j, sign):
-            k = (j * 5) % (G * G)
+            k = ((j + 1) * 5) % (G * G)
             return ring(self.z, sign * (k // G)), ring(self.y, sign * (k % G)), base + k
 
         def start(j, _):
             z, y, k = place(j, 1)
             if before is not None:
                 before(z, y)
-            self.copy(src(z, y), dst, self.dev(z=z, y=y), k).start()
+            self.copy(src(z, y), dst, self.dev(z=z, y=y, c=core), k).start()
             return _
 
         def each(fn):
             def body(j, _):
                 z, y, k = place(j, -1)
-                self.copy(dst, dst, self.dev(z=z, y=y), k).wait_recv()
+                self.copy(dst, dst, self.dev(z=z, y=y, c=core), k).wait_recv()
                 fn(z, y)
                 return _
-            lax.fori_loop(1, G * G, body, 0)
+            lax.fori_loop(0, count, body, 0)
 
         def end(j, _):
             z, y, k = place(j, 1)
-            self.copy(dst, dst, self.dev(z=z, y=y), k).wait_send()
+            self.copy(dst, dst, self.dev(z=z, y=y, c=core), k).wait_send()
             return _
 
-        lax.fori_loop(1, G * G, start, 0)
-        self.ends.append(lambda: lax.fori_loop(1, G * G, end, 0))
+        lax.fori_loop(0, count, start, 0)
+        self.ends.append(lambda: lax.fori_loop(0, count, end, 0))
         return each
 
     def peers(self):
@@ -122,14 +124,15 @@
 class RepSum:
     def __init__(self, net, terms, far, near, mid, last):
         self.net, self.terms, self.near, self.mid, self.last = net, terms, near, mid, last
-        self.size = near.shape[-T]
+        self.size, slices = near.shape[-T], near.shape[1]
+        self.slices = range(slices)
         q = self.size // T
-        self.parts = [(h, s) for s in (0, 1) for h in (0, 1)]
+        self.parts = [(h, s) for s in self.slices for h in (0, 1)]
         self.tree = {}
         for h, s in self.parts:
 
             def at(t, d, h=h, s=s):
-                row = pl.ds((h * T + s) * self.size + d * q, q)
+                row = pl.ds((h * slices + s) * self.size + d * q, q)
                 return terms.at[t, :, row] if h else terms.at[:, t, row]
 
             self.tree[h, s] = Tree(
@@ -137,11 +140,11 @@
             )
 
     def start(self, h):
-        for s in (0, 1):
+        for s in self.slices:
             self.tree[h, s].start()
 
     def free(self, h):
-        for s in (0, 1):
+        for s in self.slices:
             for d in (0, 1):
                 self.tree[h, s].free(d)
 
@@ -153,7 +156,7 @@
         for h, s in self.parts:
             tree, mid = self.tree[h, s], self.mid.at[h, s]
             tree.end()
-            row = pl.ds((h * T + s) * size, size)
+            row = pl.ds((h * len(self.slices) + s) * size, size)
             own = self.terms[tree.p, :, row] if h else self.terms[:, tree.p, row]
             mid[...] = own + self.near[h, s, 0] + self.near[h, s, 1]
             axis = "zy"[h]
@@ -165,7 +168,7 @@
             total = self.mid[h, s, p]
             for k in (1, 2, 3):
                 total = total + self.last[h, s, ring(p, k)]
-            out[pl.ds((h * T + s) * size, size)] = total
+            out[pl.ds((h * len(self.slices) + s) * size, size)] = total
 
 
 def exchange(net, axis, src, buf):
@@ -173,28 +176,43 @@
     return [net.send(src(ring(p, k)), buf.at[p], net.near(axis, k)) for k in (2, 1, 3)]
 
 
+def wait_all(copies):
+    for copy in copies:
+        copy.wait_recv()
+
+
 def gather_nodes(net, buf):
-    mine = buf.at[net.x * T + net.c]
+    node = lambda k, core: ring(net.x, k) * T + core
+    mine = buf.at[node(0, net.c)]
+    other = 1 - net.c
     out = []
     for k in (2, 1, 3):
-        out.append(net.send(mine, mine, net.near("x", k)))
-        out.append(net.send(mine, mine, net.dev(x=ring(net.x, k), c=1 - net.c)))
-    return out + [net.send(mine, mine, net.partner())]
-
-
-def gather_pairs(net, buf):
-    block = lambda k: buf.at[ring(net.x, k) * T + net.c]
-    own = block(0)
-    over = [net.send(own, own, net.partner())]
-    come = [(k, net.send(own, own, net.near("x", k))) for k in (1, 3, 2)]
+        out.append((node(-k, net.c), net.send(mine, mine, net.near("x", k))))
+        out.append((node(-k, other), net.send(mine, mine, net.dev(x=ring(net.x, k), c=other))))
+    return [(node(0, other), net.send(mine, mine, net.partner()))] + out
+
+
+def gather_pairs(net, buf, done):
+    node = lambda k, core: ring(net.x, k) * T + core
+    other = 1 - net.c
+
+    def move(n, device):
+        return net.send(buf.at[n], buf.at[n], device)
+
+    me = node(0, net.c)
+    over = [(node(0, other), move(me, net.partner()))]
+    come = [(k, move(me, net.dev(x=ring(net.x, k), c=other))) for k in (2, 1, 3)]
+    done(me)
     for k, copy in come:
         copy.wait_recv()
-        over.append(net.send(block(-k), block(-k), net.partner()))
-    for copy in over:
+        over.append((node(-k, net.c), move(node(-k, other), net.partner())))
+        done(node(-k, other))
+    for n, copy in over:
         copy.wait_recv()
-
-
-def gather_rep(net, buf):
+        done(n)
+
+
+def gather_rep(net, buf, early):
     q = buf.shape[T] // G
 
     def move(s, u, v, device, part=None):
@@ -218,6 +236,7 @@
 
     for s in state:
         cross(s, 0)
+    extra = early()
     for n in range(3):
         for s in state:
             k, copy = s["near"][n]
@@ -231,8 +250,8 @@
             last.append(move(s, u, ring(s["v"], -1), s["up"], 0))
             down.wait_recv()
             last.append(move(s, u, ring(s["v"], 1), s["down"], 1))
-    for copy in last:
-        copy.wait_recv()
+    wait_all(last)
+    return extra
 
 
 def lanes(shape):
@@ -250,17 +269,17 @@
 
 
 def scratch_shapes():
-    half, piece = HID // T, ROW // G
+    half, thin, piece = HID // T, ROW // 6, CLS + N
     return dict(
         a_v=((TALL, WIDE), BF16),
         xg=((N, ROW, LANE), BF16),
         cg=((N, N, LANE), F32),
         y1=((WIDE, HID), BF16),
         zp=((G, G, ROW, HID), F32),
-        far=((T, T, T, G, piece // T, HID), F32),
-        near=((T, T, T, G, piece, HID), F32),
-        mid=((T, T, G, piece, HID), F32),
-        last=((T, T, G, piece, HID), F32),
+        far=((T, 3, T, G, thin // T, HID), F32),
+        near=((T, 3, T, G, thin, HID), F32),
+        mid=((T, 3, G, thin, HID), F32),
+        last=((T, 3, G, thin, HID), F32),
         z1=((ROW, HID), F32),
         h1=((ROW, HID), BF16),
         w2p=((LANE, HID), F32),
@@ -268,11 +287,12 @@
         y2u=((WIDE, LANE), BF16),
         zq=((G, G, PK, LANE), F32),
         zi=((G, G, PK, LANE), F32),
+        g2s=((PK, LANE), BF16),
         g2g=((G, G, PK, LANE), BF16),
         g2u=((TALL, LANE), BF16),
-        d2=((G, piece, PAIR), F32),
-        d2i=((G, piece, PAIR), F32),
-        d2s=((T, piece, PAIR), F32),
+        d2=((G, CLS, PAIR), F32),
+        d2i=((G, CLS, PAIR), F32),
+        d2s=((T, CLS, PAIR), F32),
         d2t=((PAIR, LANE), F32),
         g1g=((G, G, ROW, HID), BF16),
         e1=((G, HID, PAIR), F32),
@@ -282,10 +302,20 @@
         e1near=((T, half, PAIR), F32),
         w2s=((T, piece, LANE), F32),
         w2o=((piece, LANE), F32),
-        ra=((G, G, G * G, LANE), F32),
-        rai=((G, G, G * G, LANE), F32),
-        rx=((G, G * G, LANE), F32),
-        rf=((T, G, G, G * G, LANE), F32),
+        wx=((G, piece, LANE), F32),
+        wr=((G, G, piece, LANE), F32),
+        wf=((T, piece, LANE), F32),
+        ra=((G, G, N, LANE), F32),
+        rai=((G, G, N, LANE), F32),
+        rx=((N, LANE), F32),
+        rxi=((G, N, LANE), F32),
+        rs=((N, LANE), F32),
+        rf=((T, G, G, N, LANE), F32),
+        w1v=((LANE, HID), F32),
+        lab=((ROW,), jnp.int32),
+        msk=((ROW,), jnp.int32),
+        lab_o=((ROW,), jnp.int32),
+        msk_o=((ROW,), jnp.int32),
     )
 
 
@@ -297,35 +327,41 @@
     z, y, x, c = net.z, net.y, net.x, net.c
     a_v = s["a_v"]
 
-    tall = [pl.ds(k * (TALL // G), TALL // G) for k in range(G)]
-    loads = [pltpu.make_async_copy(adj.at[rows], a_v.at[rows], load_sem.at[k]) for k, rows in enumerate(tall)]
-    for load in loads:
-        load.start()
-
     barrier = pltpu.get_barrier_semaphore()
     peers = net.peers()
     for peer in peers:
         pl.semaphore_signal(barrier, inc=1, device_id=peer, device_id_type=MESH)
 
     me = x * T + c
-    xg, cg = s["xg"], s["cg"]
-    xg[me] = x_ref[...]
-    mask_row = msk_ref[...].astype(F32).reshape(1, ROW)
-    label_row = lab_ref[...].reshape(1, ROW)
-    cg[me] = jnp.broadcast_to(jnp.sum(mask_row, axis=1, keepdims=True), (N, LANE))
-    w2p = s["w2p"]
+    xg, cg, w2p, w1v, y1 = (s[k] for k in ("xg", "cg", "w2p", "w1v", "y1"))
+    tall = [pl.ds(k * (TALL // G), TALL // G) for k in range(G)]
     w2p[...] = jnp.zeros((LANE, HID), F32)
-    w2p[:CLS] = w2_ref[...]
+    pairs = [(msk_ref, s["msk"]), (lab_ref, s["lab"]), (x_ref, xg.at[me]), (w1_ref, w1v), (w2_ref, w2p.at[pl.ds(0, CLS)])]
+    pairs += [(adj.at[rows], a_v.at[rows]) for rows in tall]
+    loads = [pltpu.make_async_copy(src, dst, load_sem.at[k]) for k, (src, dst) in enumerate(pairs)]
+    for load in loads:
+        load.start()
+    small = len(loads) - G
+    for load in loads[:small]:
+        load.wait()
+
+    def row_of(ref, dtype):
+        return ref[...].astype(dtype).reshape(1, ROW)
+
+    cg[me] = jnp.broadcast_to(jnp.sum(row_of(s["msk"], F32), axis=1, keepdims=True), (N, LANE))
     w2b = w2p[...].astype(BF16)
-    w1b = w1_ref[...].astype(BF16)
+    w1b = w1v[...].astype(BF16)
 
     pl.semaphore_wait(barrier, len(peers))
 
-    counts = gather_nodes(net, cg)
-    gather_pairs(net, xg)
-    y1 = s["y1"]
-    y1[...] = dot(xg[...].reshape(WIDE, LANE), w1b, 1, 0).astype(BF16)
-    for load in loads:
+    swaps = [net.send(s[k], s[k + "_o"], net.partner()) for k in ("lab", "msk")]
+    counts = [copy for _, copy in gather_nodes(net, cg)]
+
+    def y1_block(n):
+        y1[span(n * ROW, ROW)] = dot(xg[n], w1b, 1, 0).astype(BF16)
+
+    gather_pairs(net, xg, y1_block)
+    for load in loads[small:]:
         load.wait()
 
     zp = s["zp"]
@@ -357,18 +393,17 @@
     y2 = dot(h1[...], w2b, 1, 1).astype(BF16).astype(F32)
     y2g, y2u = s["y2g"], s["y2u"]
     y2g[me] = pack(y2).astype(BF16)
-    for copy in counts + gather_nodes(net, y2g):
-        copy.wait_recv()
+    blocks = gather_nodes(net, y2g)
 
     def spread(src, dst, base):
         for g, part in enumerate(unpack(src.astype(F32))):
             dst[span(base * ROW + g * PK, PK)] = part.astype(BF16)
 
-    def spread_y2(j, _):
-        spread(y2g[j], y2u, j)
-        return _
-
-    lax.fori_loop(0, N, spread_y2, 0)
+    spread(y2g[me], y2u, me)
+    wait_all(counts + swaps)
+    for n, copy in blocks:
+        copy.wait_recv()
+        spread(y2g[n], y2u, n)
 
     zq, zi = s["zq"], s["zi"]
     count = jnp.sum(cg[...], axis=0)[:1]
@@ -378,9 +413,8 @@
     def z2_block(zz, yy):
         zq[zz, yy] = pack(dot(block(zz, yy), y2u[...], 1, 0)) + count
 
-    arrivals = net.rep_all(lambda zz, yy: zq.at[zz, yy], zi.at[z, y], z2_block)
-    z2_block(z, y)
-    zi[z, y] = zq[z, y]
+    arrivals = net.rep_all(lambda zz, yy: zq.at[zz, yy], zi.at[z, y], z2_block, flip=True)
+    mask_row, label_row = row_of(s["msk_o"], F32), row_of(s["lab_o"], jnp.int32)
     mask_all = jnp.broadcast_to(mask_row, (LANE, ROW)).T
     classes = lax.broadcasted_iota(jnp.int32, (LANE, ROW), 0)
     one_hot = (jnp.broadcast_to(label_row, (LANE, ROW)) == classes).astype(F32).T
@@ -398,32 +432,34 @@
     picked = jnp.where(valid, -(mask_all * (one_hot * log_probs)), 0.0)
     loss_part = jnp.sum(picked, axis=0, keepdims=True)
     g2 = jnp.where(valid, (jnp.exp(log_probs) - one_hot) * (mask_all / total), 0.0).astype(BF16).astype(F32)
-    g2g, g2u = s["g2g"], s["g2u"]
-    g2g[z, y] = pack(g2).astype(BF16)
+    g2s, g2g, g2u = s["g2s"], s["g2g"], s["g2u"]
+    g2s[...] = pack(g2).astype(BF16)
 
     def spread_g2(zz, yy):
         spread(g2g[zz, yy], g2u, zz * G + yy)
 
-    arrivals = net.rep_all(lambda zz, yy: g2g.at[z, y], g2g.at[z, y])
-    spread_g2(z, y)
+    arrivals = net.rep_all(lambda zz, yy: g2s, g2g.at[z, y], flip=True)
     arrivals(spread_g2)
 
     d2, d2i, d2s, d2t = (s[k] for k in ("d2", "d2i", "d2s", "d2t"))
-    rows = d2.shape[1]
-
-    def d2_block(k, _):
-        part = dot(g2u[...], a_v[:, span(k * T * PAIR, T * PAIR)], 0, 0)
-        d2[T * k] = part[:rows, :PAIR]
-        d2[T * k + 1] = part[:rows, PAIR:]
-        return _
-
-    lax.fori_loop(0, T, d2_block, 0)
-    for copy in exchange(net, "x", lambda t: d2.at[t], d2i):
-        copy.wait_recv()
+
+    def d2_block(k):
+        part = dot(g2u[...], a_v[:, span(k * T * PAIR, T * PAIR)], 0, 0)[:CLS]
+        d2[T * k] = part[:, :PAIR]
+        d2[T * k + 1] = part[:, PAIR:]
+
+    def d2_send(t):
+        return net.send(d2.at[t], d2i.at[x], net.dev(x=t, c=1 - c))
+
+    d2_block(1 - x // T)
+    copies = [d2_send(ring(x, T)), d2_send(3 - x)]
+    d2_block(x // T)
+    copies.append(d2_send(x + 1 - T * (x % T)))
     d2i[x] = d2[x]
+    wait_all(copies)
     d2s[c] = jnp.sum(d2i[...], axis=0)
     net.send(d2s.at[c], d2s.at[c], net.partner()).wait_recv()
-    d2t[...] = jnp.concatenate([d2s[0] + d2s[1], jnp.zeros((LANE - rows, PAIR), F32)], axis=0).T
+    d2t[...] = jnp.concatenate([d2s[0] + d2s[1], jnp.zeros((LANE - CLS, PAIR), F32)], axis=0).T
     dy2 = d2t[span(c * ROW, ROW)].astype(BF16)
 
     dh1 = dot(dy2, w2b, 1, 0)
@@ -437,9 +473,16 @@
         w2s[h, :CLS] = dw2_t[:, h * LANE : (h + 1) * LANE]
         w2s[h, CLS:] = loss_tile
     swap = net.send(w2s.at[1 - c], w2o, net.partner())
-
-    gather_rep(net, g1g)
-    swap.wait_recv()
+    wx, wr, wf = s["wx"], s["wr"], s["wf"]
+
+    def early():
+        swap.wait_recv()
+        wx[x] = w2s[c] + w2o[...]
+        return exchange(net, "x", lambda t: wx.at[x], wx)
+
+    wait_all(gather_rep(net, g1g, early))
+    wr[z, y] = jnp.sum(wx[...], axis=0)
+    w_arrivals = net.rep_all(lambda zz, yy: wr.at[z, y], wr.at[z, y])
 
     e1, e1o, e1s, e1far, e1near = (s[k] for k in ("e1", "e1o", "e1s", "e1far", "e1near"))
     half = HID // T
@@ -468,29 +511,27 @@
     tree.free(1)
     tree.relay()
     e1_join(*own)
+    w_arrivals(lambda zz, yy: None)
+    wf[c] = jnp.sum(wr[...].reshape(G * G, CLS + N, LANE), axis=0)
+    swap = net.send(wf.at[c], wf.at[c], net.partner())
     tree.end()
     dy1 = (e1s[x] + e1near[0] + e1near[1]).astype(BF16)
     dw1_t = dot(dy1, xg[pl.ds(x * T, T)].reshape(PAIR, LANE), 1, 0)
 
-    ra, rai, rx, rf = (s[k] for k in ("ra", "rai", "rx", "rf"))
-    tile = G * G
-    ra[:T] = dw1_t.reshape(T, G, tile, LANE)
-    ra[T, :3] = (w2s[c] + w2o[...]).reshape(3, tile, LANE)
-    ra[T, 3] = jnp.zeros((tile, LANE), F32)
-    ra[3] = jnp.zeros((G, tile, LANE), F32)
-    arrivals = net.rep_all(lambda zz, yy: ra.at[zz, yy], rai.at[z, y])
-    rai[z, y] = ra[z, y]
+    ra, rai, rx, rxi, rs, rf = (s[k] for k in ("ra", "rai", "rx", "rxi", "rs", "rf"))
+    ra[...] = dw1_t.reshape(G, G, N, LANE)
+    arrivals = net.rep_all(lambda zz, yy: ra.at[zz, yy], rai.at[z, y], flip=True)
     arrivals(lambda zz, yy: None)
-    rx[x] = jnp.sum(rai[...].reshape(tile, tile, LANE), axis=0)
-    for copy in exchange(net, "x", lambda t: rx.at[x], rx):
-        copy.wait_recv()
-    rf[c, z, y] = jnp.sum(rx[...], axis=0)
-    arrivals = net.rep_all(lambda zz, yy: rf.at[c, z, y], rf.at[c, z, y])
+    rx[...] = jnp.sum(rai[...].reshape(G * G, N, LANE), axis=0)
+    wait_all([net.send(rx, rxi.at[x], net.dev(x=ring(x, k), c=1 - c)) for k in (2, 1, 3, 0)])
+    rs[...] = jnp.sum(rxi[...], axis=0)
+    arrivals = net.rep_all(lambda zz, yy: rs, rf.at[c, z, y], flip=True)
+    swap.wait_recv()
+    out_ref[:, span(LANE, CLS + N)] = wf[...]
+    out_ref[0, span(LANE + CLS + N, N)] = jnp.broadcast_to(total[:1], (N, LANE))
     arrivals(lambda zz, yy: None)
-    net.send(rf.at[c], rf.at[c], net.partner()).wait_recv()
-
-    out_ref[...] = rf[:, :3].reshape(T, 3 * G * tile, LANE)
-    out_ref[0, span(3 * G * tile - N, N)] = jnp.broadcast_to(total[:1], (N, LANE))
+    net.send(rf.at[1 - c], rf.at[1 - c], net.partner()).wait_recv()
+    out_ref[:, :LANE] = rf[...].reshape(T, LANE, LANE)
     for end in net.ends:
         end()
 
@@ -501,7 +542,7 @@
         dw1_ref[:, half] = sums[h, :LANE].T
         dw2_ref[:, half] = sums[h, LANE : LANE + CLS]
     loss = jnp.sum(sums[0, LANE + CLS : LANE + CLS + N])
-    loss_ref[0, 0] = loss / jnp.max(sums[0, sums.shape[1] - N :])
+    loss_ref[0, 0] = loss / jnp.max(sums[0, LANE + CLS + N :])
 
 
 def solution(mesh):
@@ -509,11 +550,11 @@
     struct = lambda *shape: jax.ShapeDtypeStruct(shape, F32)
 
     def device_step(adj_blk, feat_blk, w_one, w_two, label_blk, mask_blk):
-        sems = [pltpu.SemaphoreType.DMA((n,)) for n in (N_SEM, N_SEM, G)]
+        sems = [pltpu.SemaphoreType.DMA((n,)) for n in (N_SEM, N_SEM, N + 1)]
         sums = pl.pallas_call(
             kernel,
-            out_shape=struct(T, 3 * G * G * G, LANE),
-            in_specs=[pl.BlockSpec(memory_space=pl.ANY)] + [vmem] * 5,
+            out_shape=struct(T, LANE + CLS + T * N, LANE),
+            in_specs=[pl.BlockSpec(memory_space=pl.ANY)] * 6,
             out_specs=vmem,
             scratch_shapes=[pltpu.VMEM(shape, dtype) for shape, dtype in scratch_shapes().values()] + sems,
             compiler_params=pltpu.CompilerParams(collective_id=0, has_side_effects=True, vmem_limit_bytes=56 << 20),

time: 115 us -> 113 us (0.983)
  Pallas kernels: 114 us -> 112 us
    pallas_call x1, Pallas kernels: 112 us -> 111 us  [device_step(): pl.pallas_call(kernel, out_shape=struct(T, LANE + CLS + T * N, LANE), in_...]
where the time goes in v2:
time: 113 us
  Pallas kernels  112 us (99%)
    pallas_call x1, Pallas kernels, device_step(): pl.pallas_call(kernel, out_shape=struct(T, LANE + CLS + T * N, LANE), in_...  111 us

profile of v2, /device:TPU:1, one launch (start us, length us, event | category | flops | bytes accessed | tf_op | source)
XLA Modules:
  0.0 112.9 jit_solution(1698603337224828652)
XLA Ops:
  0.6 110.5 %shard_map.85.sums = f32[2,184,128]{2,1,0:T(8,128)} custom-call(bf16[3072,1536]{1,0:T(8,128)(2,1)} %bitcast.4, bf16[192,128]{1,0:T(8,128)(2,1)} %x_ref.1, f32[128,256]{1,0:T(8,128)} %w1_ref.1, f32[40,256]{1,0:T(8,128)} %bitcast.5, s32[192]{0:T(256)} %lab_ref.1, s32[192]{0:T(256)} %msk_ref.1), custom_call_target="tpu_custom_call" | custom-call | tf_op jit(solution)/shard_map/pallas_call | solution.py:554
  111.2 1.7 %shard_map.86 = (f32[1,1]{1,0:T(1,128)}, f32[128,256]{1,0:T(8,128)}, f32[40,256]{1,0:T(8,128)}) custom-call(f32[2,184,128]{2,1,0:T(8,128)} %shard_map.85.sums), custom_call_target="tpu_custom_call" | custom-call | tf_op jit(solution)/shard_map/pallas_call | solution.py:562

commit v3 on v2

--- a/solution.py
+++ b/solution.py
@@ -12,7 +12,7 @@
 PK = ROW // 3
 TALL, WIDE = 16 * ROW, N * ROW
 PAIR = T * ROW
-N_SEM = 320
+N_SEND, N_RECV = 61, 90
 
 
 def ring(v, k):
@@ -31,7 +31,8 @@
     def __init__(self, send_sem, recv_sem):
         rep, node = lax.axis_index("rep"), lax.axis_index("nodes")
         self.z, self.y, self.x, self.c = rep // G, rep % G, node // T, node % T
-        self.sems, self.used, self.ends = (send_sem, recv_sem), 0, []
+        self.send_sem, self.recv_sem = send_sem, recv_sem
+        self.used, self.spare, self.ends = 0, [], []
 
     def dev(self, **place):
         z, y, x, c = (place.get(k, getattr(self, k)) for k in "zyxc")
@@ -43,49 +44,45 @@
     def partner(self):
         return self.dev(c=1 - self.c)
 
-    def copy(self, src, dst, device, k):
-        send, recv = (sem.at[k] for sem in self.sems)
+    def recv_index(self):
+        if self.spare:
+            return self.spare.pop()
+        self.used += 1
+        return self.used - 1
+
+    def copy(self, src, dst, device, k, n):
+        send, recv = self.send_sem.at[k], self.recv_sem.at[n]
         return pltpu.make_async_remote_copy(src_ref=src, dst_ref=dst, send_sem=send, recv_sem=recv, device_id=device, device_id_type=MESH)
 
     def send(self, src, dst, device):
-        copy = self.copy(src, dst, device, self.used)
-        self.used += 1
+        copy = self.copy(src, dst, device, len(self.ends), self.recv_index())
         copy.start()
-        self.ends.append(copy.wait_send)
+        self.ends.append(copy)
         return copy
 
-    def rep_all(self, src, dst, before=None, flip=False):
-        base, self.used = self.used, self.used + G * G
-        count = G * G if flip else G * G - 1
-        core = 1 - self.c if flip else self.c
-
-        def place(j, sign):
-            k = ((j + 1) * 5) % (G * G)
-            return ring(self.z, sign * (k // G)), ring(self.y, sign * (k % G)), base + k
-
-        def start(j, _):
-            z, y, k = place(j, 1)
-            if before is not None:
-                before(z, y)
-            self.copy(src(z, y), dst, self.dev(z=z, y=y, c=core), k).start()
-            return _
-
-        def each(fn):
-            def body(j, _):
-                z, y, k = place(j, -1)
-                self.copy(dst, dst, self.dev(z=z, y=y, c=core), k).wait_recv()
-                fn(z, y)
-                return _
-            lax.fori_loop(0, count, body, 0)
-
-        def end(j, _):
-            z, y, k = place(j, 1)
-            self.copy(dst, dst, self.dev(z=z, y=y, c=core), k).wait_send()
-            return _
-
-        lax.fori_loop(0, count, start, 0)
-        self.ends.append(lambda: lax.fori_loop(0, count, end, 0))
-        return each
+    def flush(self):
+        for copy in self.ends:
+            copy.wait_send()
+        self.ends = []
+
+    def rep_all(self, src, buf):
+        k, n = len(self.ends), self.recv_index()
+        mine = buf.at[self.z, self.y]
+        whole = self.copy(buf, buf, self.partner(), k, n)
+        self.ends.append(whole)
+
+        def start(dz, dy):
+            z, y = ring(self.z, dz), ring(self.y, dy)
+            self.copy(src(z, y), mine, self.dev(z=z, y=y, c=1 - self.c), k, n).start()
+
+        return start, whole
+
+    def rep_send(self, src, buf):
+        start, whole = self.rep_all(src, buf)
+        for j in range(G * G):
+            k = (j + 1) * 5 % (G * G)
+            start(k // G, k % G)
+        return whole
 
     def peers(self):
         out = [self.partner()]
@@ -143,10 +140,9 @@
         for s in self.slices:
             self.tree[h, s].start()
 
-    def free(self, h):
+    def free(self, h, d):
         for s in self.slices:
-            for d in (0, 1):
-                self.tree[h, s].free(d)
+            self.tree[h, s].free(d)
 
     def finish(self, out):
         net, size = self.net, self.size
@@ -212,14 +208,17 @@
         done(n)
 
 
-def gather_rep(net, buf, early):
+def gather_rep(net, buf, early, spare):
     q = buf.shape[T] // G
 
     def move(s, u, v, device, part=None):
         h = s["h"]
         row = pl.ds(h * T * q, T * q) if part is None else pl.ds((h * T + part) * q, q)
         ref = buf.at[u, v, row] if h else buf.at[v, u, row]
-        return net.send(ref, ref, device)
+        net.spare = spare
+        copy = net.send(ref, ref, device)
+        net.spare = []
+        return copy
 
     state = []
     for h in (0, 1):
@@ -236,12 +235,13 @@
 
     for s in state:
         cross(s, 0)
-    extra = early()
+    later = early()
     for n in range(3):
         for s in state:
             k, copy = s["near"][n]
             copy.wait_recv()
             cross(s, -k)
+    extra = later()
     last = []
     for n in range(G):
         for s in state:
@@ -269,17 +269,17 @@
 
 
 def scratch_shapes():
-    half, thin, piece = HID // T, ROW // 6, CLS + N
+    half, thin, piece = HID // T, ROW // G, CLS + N
     return dict(
-        a_v=((TALL, WIDE), BF16),
+        a_v=((G, G, ROW, WIDE), BF16),
         xg=((N, ROW, LANE), BF16),
         cg=((N, N, LANE), F32),
         y1=((WIDE, HID), BF16),
         zp=((G, G, ROW, HID), F32),
-        far=((T, 3, T, G, thin // T, HID), F32),
-        near=((T, 3, T, G, thin, HID), F32),
-        mid=((T, 3, G, thin, HID), F32),
-        last=((T, 3, G, thin, HID), F32),
+        far=((T, T, T, G, thin // T, HID), F32),
+        near=((T, T, T, G, thin, HID), F32),
+        mid=((T, T, G, thin, HID), F32),
+        last=((T, T, G, thin, HID), F32),
         z1=((ROW, HID), F32),
         h1=((ROW, HID), BF16),
         w2p=((LANE, HID), F32),
@@ -303,6 +303,7 @@
         w2s=((T, piece, LANE), F32),
         w2o=((piece, LANE), F32),
         wx=((G, piece, LANE), F32),
+        wr_own=((piece, LANE), F32),
         wr=((G, G, piece, LANE), F32),
         wf=((T, piece, LANE), F32),
         ra=((G, G, N, LANE), F32),
@@ -334,10 +335,9 @@
 
     me = x * T + c
     xg, cg, w2p, w1v, y1 = (s[k] for k in ("xg", "cg", "w2p", "w1v", "y1"))
-    tall = [pl.ds(k * (TALL // G), TALL // G) for k in range(G)]
     w2p[...] = jnp.zeros((LANE, HID), F32)
     pairs = [(msk_ref, s["msk"]), (lab_ref, s["lab"]), (x_ref, xg.at[me]), (w1_ref, w1v), (w2_ref, w2p.at[pl.ds(0, CLS)])]
-    pairs += [(adj.at[rows], a_v.at[rows]) for rows in tall]
+    pairs += [(adj.at[k], a_v.at[k]) for k in range(G)]
     loads = [pltpu.make_async_copy(src, dst, load_sem.at[k]) for k, (src, dst) in enumerate(pairs)]
     for load in loads:
         load.start()
@@ -366,27 +366,28 @@
 
     zp = s["zp"]
 
-    def block(zz, yy):
-        return a_v[span((zz * G + yy) * ROW, ROW)]
-
-    def z1_loop(count, place):
-        def body(k, _):
-            zz, yy = place(k)
-            zp[zz, yy] = dot(block(zz, yy), y1[...], 1, 0)
-            return _
-        lax.fori_loop(0, count, body, 0)
-
     sum1 = RepSum(net, zp, s["far"], s["near"], s["mid"], s["last"])
-    z1_loop(G, lambda k: (k, ring(y, 2)))
-    sum1.start(0)
-    z1_loop(3, lambda k: (ring(z, 2), ring(y, k - 1)))
-    sum1.start(1)
-    z1_loop(6, lambda k: (ring(z, k // 2 - 1), ring(y, 1 + 2 * (k % 2))))
-    sum1.free(0)
-    z1_loop(3, lambda k: (ring(z, k - 1), y))
-    sum1.free(1)
+
+    def z1_block(h, t):
+        row = pl.ds(h * ROW // T, ROW // T)
+        a = a_v[t, :, row] if h else a_v[:, t, row]
+        term = dot(a.reshape(TALL // N, WIDE), y1[...], 1, 0).reshape(G, ROW // T, HID)
+        if h:
+            zp[t, :, row] = term
+        else:
+            zp[:, t, row] = term
+
+    base = net.used
+    for k in (2, 1, 3, 0):
+        for h, p in enumerate((y, z)):
+            z1_block(h, ring(p, k))
+            if k == T:
+                sum1.start(h)
+            elif k > 0:
+                sum1.free(h, k // T)
     z1 = s["z1"]
     sum1.finish(z1)
+    z1_used = list(range(base, net.used))
 
     h1 = s["h1"]
     h1[...] = jnp.maximum(z1[...], 0.0).astype(BF16)
@@ -399,26 +400,36 @@
         for g, part in enumerate(unpack(src.astype(F32))):
             dst[span(base * ROW + g * PK, PK)] = part.astype(BF16)
 
-    spread(y2g[me], y2u, me)
-    wait_all(counts + swaps)
-    for n, copy in blocks:
-        copy.wait_recv()
-        spread(y2g[n], y2u, n)
+    def spread_y2(j, _):
+        spread(y2g[j], y2u, j)
+        return _
+
+    wait_all(counts + swaps + [copy for _, copy in blocks])
+    lax.fori_loop(0, N, spread_y2, 0)
+    net.flush()
 
     zq, zi = s["zq"], s["zi"]
     count = jnp.sum(cg[...], axis=0)[:1]
     at_count = lanes((PK, LANE)) == 3 * CLS
     count = jnp.where(at_count, jnp.broadcast_to(count, (PK, LANE)), 0.0)
 
-    def z2_block(zz, yy):
-        zq[zz, yy] = pack(dot(block(zz, yy), y2u[...], 1, 0)) + count
-
-    arrivals = net.rep_all(lambda zz, yy: zq.at[zz, yy], zi.at[z, y], z2_block, flip=True)
+    start, arrivals = net.rep_all(lambda zz, yy: zq.at[zz, yy], zi)
+
+    def z2_blocks(j, _):
+        dz, p = j // T + 1, T * (j % T)
+        zz = ring(z, dz)
+        term = dot(a_v[zz, pl.ds(p, T)].reshape(PAIR, WIDE), y2u[...], 1, 0)
+        for k in (0, 1):
+            zq[zz, p + k] = pack(term[k * ROW : (k + 1) * ROW]) + count
+            start(dz, p + k - y)
+        return _
+
+    lax.fori_loop(0, N, z2_blocks, 0)
     mask_row, label_row = row_of(s["msk_o"], F32), row_of(s["lab_o"], jnp.int32)
     mask_all = jnp.broadcast_to(mask_row, (LANE, ROW)).T
     classes = lax.broadcasted_iota(jnp.int32, (LANE, ROW), 0)
     one_hot = (jnp.broadcast_to(label_row, (LANE, ROW)) == classes).astype(F32).T
-    arrivals(lambda zz, yy: None)
+    arrivals.wait_recv()
     packed = jnp.sum(zi[...].reshape(G * G, PK, LANE), axis=0)
 
     total = jnp.sum(jnp.where(at_count, packed, 0.0), axis=1, keepdims=True)
@@ -435,16 +446,20 @@
     g2s, g2g, g2u = s["g2s"], s["g2g"], s["g2u"]
     g2s[...] = pack(g2).astype(BF16)
 
-    def spread_g2(zz, yy):
-        spread(g2g[zz, yy], g2u, zz * G + yy)
-
-    arrivals = net.rep_all(lambda zz, yy: g2s, g2g.at[z, y], flip=True)
-    arrivals(spread_g2)
+    def spread_g2(k, _):
+        spread(g2g[k // G, k % G], g2u, k)
+        return _
+
+    net.rep_send(lambda zz, yy: g2s, g2g).wait_recv()
+    lax.fori_loop(0, G * G, spread_g2, 0)
 
     d2, d2i, d2s, d2t = (s[k] for k in ("d2", "d2i", "d2s", "d2t"))
 
+    def a_cols(k, size):
+        return a_v[:, :, :, span(k * size, size)].reshape(TALL, size)
+
     def d2_block(k):
-        part = dot(g2u[...], a_v[:, span(k * T * PAIR, T * PAIR)], 0, 0)[:CLS]
+        part = dot(g2u[...], a_cols(k, T * PAIR), 0, 0)[:CLS]
         d2[T * k] = part[:, :PAIR]
         d2[T * k + 1] = part[:, PAIR:]
 
@@ -466,23 +481,25 @@
     g1g = s["g1g"]
     g1g[z, y] = jnp.where(z1[...] > 0.0, dh1, 0.0).astype(BF16)
 
-    dw2_t = dot(dy2, h1[...], 0, 0)[:CLS]
+    w2s, w2o, wx, wr, wf = (s[k] for k in ("w2s", "w2o", "wx", "wr", "wf"))
     loss_tile = jnp.concatenate([loss_part, jnp.zeros((N - 1, LANE), F32)], axis=0)
-    w2s, w2o = s["w2s"], s["w2o"]
-    for h in (0, 1):
-        w2s[h, :CLS] = dw2_t[:, h * LANE : (h + 1) * LANE]
-        w2s[h, CLS:] = loss_tile
-    swap = net.send(w2s.at[1 - c], w2o, net.partner())
-    wx, wr, wf = s["wx"], s["wr"], s["wf"]
 
     def early():
-        swap.wait_recv()
-        wx[x] = w2s[c] + w2o[...]
-        return exchange(net, "x", lambda t: wx.at[x], wx)
-
-    wait_all(gather_rep(net, g1g, early))
-    wr[z, y] = jnp.sum(wx[...], axis=0)
-    w_arrivals = net.rep_all(lambda zz, yy: wr.at[z, y], wr.at[z, y])
+        dw2_t = dot(dy2, h1[...], 0, 0)[:CLS]
+        for h in (0, 1):
+            w2s[h, :CLS] = dw2_t[:, h * LANE : (h + 1) * LANE]
+            w2s[h, CLS:] = loss_tile
+        swap = net.send(w2s.at[1 - c], w2o, net.partner())
+
+        def later():
+            swap.wait_recv()
+            wx[x] = w2s[c] + w2o[...]
+            return exchange(net, "x", lambda t: wx.at[x], wx)
+
+        return later
+
+    net.flush()
+    swaps = gather_rep(net, g1g, early, z1_used)
 
     e1, e1o, e1s, e1far, e1near = (s[k] for k in ("e1", "e1o", "e1s", "e1far", "e1near"))
     half = HID // T
@@ -492,7 +509,7 @@
 
     def e1_block(k):
         t = ring(x, k)
-        e1[t] = dot(g1g[...].reshape(TALL, HID), a_v[:, span(t * PAIR, PAIR)], 0, 0)
+        e1[t] = dot(g1g[...].reshape(TALL, HID), a_cols(t, PAIR), 0, 0)
         return t, net.send(e1.at[t, span((1 - c) * half, half)], e1o.at[t], net.partner())
 
     def e1_join(t, copy):
@@ -506,34 +523,37 @@
     left = e1_block(3)
     e1_join(*right)
     tree.free(0)
+    wait_all(swaps)
+    wr_own = s["wr_own"]
+    wr_own[...] = jnp.sum(wx[...], axis=0)
+    w_arrivals = net.rep_send(lambda zz, yy: wr_own, wr)
     own = e1_block(0)
     e1_join(*left)
     tree.free(1)
     tree.relay()
     e1_join(*own)
-    w_arrivals(lambda zz, yy: None)
-    wf[c] = jnp.sum(wr[...].reshape(G * G, CLS + N, LANE), axis=0)
-    swap = net.send(wf.at[c], wf.at[c], net.partner())
     tree.end()
     dy1 = (e1s[x] + e1near[0] + e1near[1]).astype(BF16)
     dw1_t = dot(dy1, xg[pl.ds(x * T, T)].reshape(PAIR, LANE), 1, 0)
 
     ra, rai, rx, rxi, rs, rf = (s[k] for k in ("ra", "rai", "rx", "rxi", "rs", "rf"))
     ra[...] = dw1_t.reshape(G, G, N, LANE)
-    arrivals = net.rep_all(lambda zz, yy: ra.at[zz, yy], rai.at[z, y], flip=True)
-    arrivals(lambda zz, yy: None)
+    arrivals = net.rep_send(lambda zz, yy: ra.at[zz, yy], rai)
+    w_arrivals.wait_recv()
+    wf[1 - c] = jnp.sum(wr[...].reshape(G * G, CLS + N, LANE), axis=0)
+    swap = net.send(wf.at[1 - c], wf.at[1 - c], net.partner())
+    arrivals.wait_recv()
     rx[...] = jnp.sum(rai[...].reshape(G * G, N, LANE), axis=0)
     wait_all([net.send(rx, rxi.at[x], net.dev(x=ring(x, k), c=1 - c)) for k in (2, 1, 3, 0)])
     rs[...] = jnp.sum(rxi[...], axis=0)
-    arrivals = net.rep_all(lambda zz, yy: rs, rf.at[c, z, y], flip=True)
+    arrivals = net.rep_send(lambda zz, yy: rs, rf.at[c])
     swap.wait_recv()
     out_ref[:, span(LANE, CLS + N)] = wf[...]
     out_ref[0, span(LANE + CLS + N, N)] = jnp.broadcast_to(total[:1], (N, LANE))
-    arrivals(lambda zz, yy: None)
+    arrivals.wait_recv()
     net.send(rf.at[1 - c], rf.at[1 - c], net.partner()).wait_recv()
     out_ref[:, :LANE] = rf[...].reshape(T, LANE, LANE)
-    for end in net.ends:
-        end()
+    net.flush()
 
 
 def unpack_kernel(sums, loss_ref, dw1_ref, dw2_ref):
@@ -550,7 +570,7 @@
     struct = lambda *shape: jax.ShapeDtypeStruct(shape, F32)
 
     def device_step(adj_blk, feat_blk, w_one, w_two, label_blk, mask_blk):
-        sems = [pltpu.SemaphoreType.DMA((n,)) for n in (N_SEM, N_SEM, N + 1)]
+        sems = [pltpu.SemaphoreType.DMA((n,)) for n in (N_SEND, N_RECV, N + 1)]
         sums = pl.pallas_call(
             kernel,
             out_shape=struct(T, LANE + CLS + T * N, LANE),
@@ -558,7 +578,7 @@
             out_specs=vmem,
             scratch_shapes=[pltpu.VMEM(shape, dtype) for shape, dtype in scratch_shapes().values()] + sems,
             compiler_params=pltpu.CompilerParams(collective_id=0, has_side_effects=True, vmem_limit_bytes=56 << 20),
-        )(adj_blk.reshape(TALL, WIDE), feat_blk, w_one, w_two.T, label_blk, mask_blk)
+        )(adj_blk.reshape(G, G, ROW, WIDE), feat_blk, w_one, w_two.T, label_blk, mask_blk)
         loss, dw1, dw2 = pl.pallas_call(
             unpack_kernel,
             out_shape=(struct(1, 1), struct(LANE, HID), struct(CLS, HID)),

time: 113 us -> 108 us (0.956)
  Pallas kernels: 112 us -> 107 us
    pallas_call x1, Pallas kernels: 111 us -> 105 us  [device_step(): pl.pallas_call(kernel, out_shape=struct(T, LANE + CLS + T * N, LANE), in_...]
where the time goes in v3:
time: 108 us
  Pallas kernels  107 us (99%)
    pallas_call x1, Pallas kernels, device_step(): pl.pallas_call(kernel, out_shape=struct(T, LANE + CLS + T * N, LANE), in_...  105 us

profile of v3, /device:TPU:1, one launch (start us, length us, event | category | flops | bytes accessed | tf_op | source)
XLA Modules:
  0.0 107.9 jit_solution(2929898133859824556)
XLA Ops:
  0.6 105.5 %shard_map.85.sums = f32[2,184,128]{2,1,0:T(8,128)} custom-call(bf16[4,4,192,1536]{3,2,1,0:T(8,128)(2,1)} %bitcast.4, bf16[192,128]{1,0:T(8,128)(2,1)} %x_ref.1, f32[128,256]{1,0:T(8,128)} %w1_ref.1, f32[40,256]{1,0:T(8,128)} %bitcast.5, s32[192]{0:T(256)} %lab_ref.1, s32[192]{0:T(256)} %msk_ref.1), custom_call_target="tpu_custom_call" | custom-call | tf_op jit(solution)/shard_map/pallas_call | solution.py:574
  106.1 1.7 %shard_map.86 = (f32[1,1]{1,0:T(1,128)}, f32[128,256]{1,0:T(8,128)}, f32[40,256]{1,0:T(8,128)}) custom-call(f32[2,184,128]{2,1,0:T(8,128)} %shard_map.85.sums), custom_call_target="tpu_custom_call" | custom-call | tf_op jit(solution)/shard_map/pallas_call | solution.py:582

commit v4 on v3

--- a/solution.py
+++ b/solution.py
@@ -12,7 +12,7 @@
 PK = ROW // 3
 TALL, WIDE = 16 * ROW, N * ROW
 PAIR = T * ROW
-N_SEND, N_RECV = 61, 90
+N_SEND, N_RECV = 92, 156
 
 
 def ring(v, k):
@@ -64,6 +64,27 @@
         for copy in self.ends:
             copy.wait_send()
         self.ends = []
+
+    def rep_each(self, src, buf):
+        k, n = len(self.ends), self.used
+        self.used += G * G
+        mine = buf.at[self.z, self.y]
+        self.ends.append(self.copy(buf, buf, self.partner(), k, n))
+        for j in range(G * G):
+            m = (j + 1) * 5 % (G * G)
+            z, y = ring(self.z, m // G), ring(self.y, m % G)
+            self.copy(src, mine, self.dev(z=z, y=y, c=1 - self.c), k, n + m).start()
+
+        def each(fn):
+            def body(j, _):
+                m = (j + 1) * 5 % (G * G)
+                self.copy(mine, mine, self.partner(), k, n + m).wait_recv()
+                fn(ring(self.z, -(m // G)), ring(self.y, -(m % G)))
+                return _
+
+            lax.fori_loop(0, G * G, body, 0)
+
+        return each
 
     def rep_all(self, src, buf):
         k, n = len(self.ends), self.recv_index()
@@ -188,7 +209,7 @@
     return [(node(0, other), net.send(mine, mine, net.partner()))] + out
 
 
-def gather_pairs(net, buf, done):
+def gather_pairs(net, buf, done, extra):
     node = lambda k, core: ring(net.x, k) * T + core
     other = 1 - net.c
 
@@ -198,6 +219,7 @@
     me = node(0, net.c)
     over = [(node(0, other), move(me, net.partner()))]
     come = [(k, move(me, net.dev(x=ring(net.x, k), c=other))) for k in (2, 1, 3)]
+    out = extra()
     done(me)
     for k, copy in come:
         copy.wait_recv()
@@ -206,52 +228,28 @@
     for n, copy in over:
         copy.wait_recv()
         done(n)
-
-
-def gather_rep(net, buf, early, spare):
-    q = buf.shape[T] // G
-
-    def move(s, u, v, device, part=None):
-        h = s["h"]
-        row = pl.ds(h * T * q, T * q) if part is None else pl.ds((h * T + part) * q, q)
-        ref = buf.at[u, v, row] if h else buf.at[v, u, row]
-        net.spare = spare
-        copy = net.send(ref, ref, device)
-        net.spare = []
-        return copy
-
-    state = []
-    for h in (0, 1):
-        first, second = ("y", "z") if h == 0 else ("z", "y")
-        p, v = getattr(net, first), getattr(net, second)
-        s = dict(h=h, p=p, v=v, up=net.near(second, 1), down=net.near(second, -1), over=[])
-        s["near"] = [(k, move(s, p, v, net.near(first, k))) for k in (1, 3)]
-        s["near"].append((T, move(s, p, v, net.near(first, T))))
-        state.append(s)
-
-    def cross(s, k):
-        u = ring(s["p"], k)
-        s["over"].append((u, move(s, u, s["v"], s["up"]), move(s, u, s["v"], s["down"])))
-
-    for s in state:
-        cross(s, 0)
-    later = early()
-    for n in range(3):
-        for s in state:
-            k, copy = s["near"][n]
-            copy.wait_recv()
-            cross(s, -k)
-    extra = later()
-    last = []
-    for n in range(G):
-        for s in state:
-            u, up, down = s["over"][n]
-            up.wait_recv()
-            last.append(move(s, u, ring(s["v"], -1), s["up"], 0))
-            down.wait_recv()
-            last.append(move(s, u, ring(s["v"], 1), s["down"], 1))
-    wait_all(last)
-    return extra
+    return out
+
+
+class Spread:
+    def __init__(self, net, buf):
+        self.net, self.buf = net, buf
+        self.first = [self.along(h, "yz"[h], net.z, net.y) for h in (0, 1)]
+        self.rest = [copy for h in (0, 1) for _, copy in self.along(h, "zy"[h], net.z, net.y)]
+
+    def along(self, h, axis, z, y):
+        size = self.buf.shape[T] // T
+        ref = self.buf.at[z, y, pl.ds(h * size, size)]
+        return [(k, self.net.send(ref, ref, self.net.near(axis, k))) for k in (2, 1, 3)]
+
+    def second(self):
+        net = self.net
+        for n in range(3):
+            for h in (0, 1):
+                k, copy = self.first[h][n]
+                copy.wait_recv()
+                z, y = (ring(net.z, -k), net.y) if h else (net.z, ring(net.y, -k))
+                self.rest += [copy for _, copy in self.along(h, "zy"[h], z, y)]
 
 
 def lanes(shape):
@@ -269,17 +267,17 @@
 
 
 def scratch_shapes():
-    half, thin, piece = HID // T, ROW // G, CLS + N
+    half, thin, piece = HID // T, ROW // 6, CLS + N
     return dict(
         a_v=((G, G, ROW, WIDE), BF16),
         xg=((N, ROW, LANE), BF16),
         cg=((N, N, LANE), F32),
         y1=((WIDE, HID), BF16),
         zp=((G, G, ROW, HID), F32),
-        far=((T, T, T, G, thin // T, HID), F32),
-        near=((T, T, T, G, thin, HID), F32),
-        mid=((T, T, G, thin, HID), F32),
-        last=((T, T, G, thin, HID), F32),
+        far=((T, 3, T, G, thin // T, HID), F32),
+        near=((T, 3, T, G, thin, HID), F32),
+        mid=((T, 3, G, thin, HID), F32),
+        last=((T, 3, G, thin, HID), F32),
         z1=((ROW, HID), F32),
         h1=((ROW, HID), BF16),
         w2p=((LANE, HID), F32),
@@ -295,10 +293,13 @@
         d2s=((T, CLS, PAIR), F32),
         d2t=((PAIR, LANE), F32),
         g1g=((G, G, ROW, HID), BF16),
+        mg=((G, G, ROW, HID), BF16),
+        dys=((PK, LANE), BF16),
+        dyg=((G, G, PK, LANE), BF16),
         e1=((G, HID, PAIR), F32),
         e1o=((G, half, PAIR), F32),
         e1s=((G, half, PAIR), F32),
-        e1far=((T, half // T, PAIR), F32),
+        e1far=((T, T, half // G, PAIR), F32),
         e1near=((T, half, PAIR), F32),
         w2s=((T, piece, LANE), F32),
         w2o=((piece, LANE), F32),
@@ -354,13 +355,14 @@
 
     pl.semaphore_wait(barrier, len(peers))
 
-    swaps = [net.send(s[k], s[k + "_o"], net.partner()) for k in ("lab", "msk")]
-    counts = [copy for _, copy in gather_nodes(net, cg)]
-
     def y1_block(n):
         y1[span(n * ROW, ROW)] = dot(xg[n], w1b, 1, 0).astype(BF16)
 
-    gather_pairs(net, xg, y1_block)
+    def small_copies():
+        swaps = [net.send(s[k], s[k + "_o"], net.partner()) for k in ("lab", "msk")]
+        return swaps + [copy for _, copy in gather_nodes(net, cg)]
+
+    counts = gather_pairs(net, xg, y1_block, small_copies)
     for load in loads[small:]:
         load.wait()
 
@@ -395,6 +397,9 @@
     y2g, y2u = s["y2g"], s["y2u"]
     y2g[me] = pack(y2).astype(BF16)
     blocks = gather_nodes(net, y2g)
+    mg = s["mg"]
+    mg[z, y] = jnp.where(z1[...] > 0.0, 1.0, 0.0).astype(BF16)
+    masks = Spread(net, mg)
 
     def spread(src, dst, base):
         for g, part in enumerate(unpack(src.astype(F32))):
@@ -404,9 +409,8 @@
         spread(y2g[j], y2u, j)
         return _
 
-    wait_all(counts + swaps + [copy for _, copy in blocks])
+    wait_all(counts + [copy for _, copy in blocks])
     lax.fori_loop(0, N, spread_y2, 0)
-    net.flush()
 
     zq, zi = s["zq"], s["zi"]
     count = jnp.sum(cg[...], axis=0)[:1]
@@ -430,6 +434,7 @@
     classes = lax.broadcasted_iota(jnp.int32, (LANE, ROW), 0)
     one_hot = (jnp.broadcast_to(label_row, (LANE, ROW)) == classes).astype(F32).T
     arrivals.wait_recv()
+    net.flush()
     packed = jnp.sum(zi[...].reshape(G * G, PK, LANE), axis=0)
 
     total = jnp.sum(jnp.where(at_count, packed, 0.0), axis=1, keepdims=True)
@@ -446,12 +451,11 @@
     g2s, g2g, g2u = s["g2s"], s["g2g"], s["g2u"]
     g2s[...] = pack(g2).astype(BF16)
 
-    def spread_g2(k, _):
-        spread(g2g[k // G, k % G], g2u, k)
-        return _
-
-    net.rep_send(lambda zz, yy: g2s, g2g).wait_recv()
-    lax.fori_loop(0, G * G, spread_g2, 0)
+    arrivals = net.rep_each(g2s, g2g)
+    net.spare = z1_used
+    masks.second()
+    net.spare = []
+    arrivals(lambda zz, yy: spread(g2g[zz, yy], g2u, zz * G + yy))
 
     d2, d2i, d2s, d2t = (s[k] for k in ("d2", "d2i", "d2s", "d2t"))
 
@@ -475,37 +479,41 @@
     d2s[c] = jnp.sum(d2i[...], axis=0)
     net.send(d2s.at[c], d2s.at[c], net.partner()).wait_recv()
     d2t[...] = jnp.concatenate([d2s[0] + d2s[1], jnp.zeros((LANE - CLS, PAIR), F32)], axis=0).T
+
+    dys, dyg, g1g = s["dys"], s["dyg"], s["g1g"]
+    dys[...] = pack(d2t[span((1 - c) * ROW, ROW)].astype(BF16).astype(F32)).astype(BF16)
+    arrivals = net.rep_each(dys, dyg)
+
+    w2s, w2o, wx, wr, wf = (s[k] for k in ("w2s", "w2o", "wx", "wr", "wf"))
     dy2 = d2t[span(c * ROW, ROW)].astype(BF16)
-
-    dh1 = dot(dy2, w2b, 1, 0)
-    g1g = s["g1g"]
-    g1g[z, y] = jnp.where(z1[...] > 0.0, dh1, 0.0).astype(BF16)
-
-    w2s, w2o, wx, wr, wf = (s[k] for k in ("w2s", "w2o", "wx", "wr", "wf"))
+    dw2_t = dot(dy2, h1[...], 0, 0)[:CLS]
     loss_tile = jnp.concatenate([loss_part, jnp.zeros((N - 1, LANE), F32)], axis=0)
-
-    def early():
-        dw2_t = dot(dy2, h1[...], 0, 0)[:CLS]
-        for h in (0, 1):
-            w2s[h, :CLS] = dw2_t[:, h * LANE : (h + 1) * LANE]
-            w2s[h, CLS:] = loss_tile
-        swap = net.send(w2s.at[1 - c], w2o, net.partner())
-
-        def later():
-            swap.wait_recv()
-            wx[x] = w2s[c] + w2o[...]
-            return exchange(net, "x", lambda t: wx.at[x], wx)
-
-        return later
-
+    for h in (0, 1):
+        w2s[h, :CLS] = dw2_t[:, h * LANE : (h + 1) * LANE]
+        w2s[h, CLS:] = loss_tile
+    swap = net.send(w2s.at[1 - c], w2o, net.partner())
+    wait_all(masks.rest)
+    swap.wait_recv()
+    wx[x] = w2s[c] + w2o[...]
+    swaps = exchange(net, "x", lambda t: wx.at[x], wx)
+
+    def g1_block(zz, yy):
+        dy = jnp.concatenate(unpack(dyg[zz, yy].astype(F32)), axis=0).astype(BF16)
+        dh1 = dot(dy, w2b, 1, 0)
+        g1g[zz, yy] = jnp.where(mg[zz, yy].astype(F32) > 0.0, dh1, 0.0).astype(BF16)
+
+    arrivals(g1_block)
     net.flush()
-    swaps = gather_rep(net, g1g, early, z1_used)
 
     e1, e1o, e1s, e1far, e1near = (s[k] for k in ("e1", "e1o", "e1s", "e1far", "e1near"))
     half = HID // T
-    q = half // T
-    part = lambda d: pl.ds(d * q, q)
-    tree = Tree(net, "x", lambda t, d: e1s.at[t, part(d)], lambda d: e1far.at[d], lambda d, e: e1near.at[d, part(e)])
+    q = half // G
+
+    def tree_of(n):
+        part = lambda d: pl.ds((T * n + d) * q, q)
+        return Tree(net, "x", lambda t, d: e1s.at[t, part(d)], lambda d: e1far.at[n, d], lambda d, e: e1near.at[d, part(e)])
+
+    trees = [tree_of(n) for n in (0, 1)]
 
     def e1_block(k):
         t = ring(x, k)
@@ -519,20 +527,25 @@
     opposite = e1_block(2)
     right = e1_block(1)
     e1_join(*opposite)
-    tree.start()
+    for tree in trees:
+        tree.start()
     left = e1_block(3)
     e1_join(*right)
-    tree.free(0)
+    for tree in trees:
+        tree.free(0)
+    own = e1_block(0)
+    e1_join(*left)
+    for tree in trees:
+        tree.free(1)
+    e1_join(*own)
+    for tree in trees:
+        tree.relay()
     wait_all(swaps)
     wr_own = s["wr_own"]
     wr_own[...] = jnp.sum(wx[...], axis=0)
     w_arrivals = net.rep_send(lambda zz, yy: wr_own, wr)
-    own = e1_block(0)
-    e1_join(*left)
-    tree.free(1)
-    tree.relay()
-    e1_join(*own)
-    tree.end()
+    for tree in trees:
+        tree.end()
     dy1 = (e1s[x] + e1near[0] + e1near[1]).astype(BF16)
     dw1_t = dot(dy1, xg[pl.ds(x * T, T)].reshape(PAIR, LANE), 1, 0)
 

time: 108 us -> 103 us (0.954)
  Pallas kernels: 107 us -> 103 us
    pallas_call x1, Pallas kernels: 105 us -> 101 us  [device_step(): pl.pallas_call(kernel, out_shape=struct(T, LANE + CLS + T * N, LANE), in_...]
where the time goes in v4:
time: 103 us
  Pallas kernels  103 us (100%)
    pallas_call x1, Pallas kernels, device_step(): pl.pallas_call(kernel, out_shape=struct(T, LANE + CLS + T * N, LANE), in_...  101 us

profile of v4, /device:TPU:1, one launch (start us, length us, event | category | flops | bytes accessed | tf_op | source)
XLA Modules:
  0.0 103.3 jit_solution(6072586008570764835)
XLA Ops:
  0.6 100.9 %shard_map.85.sums = f32[2,184,128]{2,1,0:T(8,128)} custom-call(bf16[4,4,192,1536]{3,2,1,0:T(8,128)(2,1)} %bitcast.4, bf16[192,128]{1,0:T(8,128)(2,1)} %x_ref.1, f32[128,256]{1,0:T(8,128)} %w1_ref.1, f32[40,256]{1,0:T(8,128)} %bitcast.5, s32[192]{0:T(256)} %lab_ref.1, s32[192]{0:T(256)} %msk_ref.1), custom_call_target="tpu_custom_call" | custom-call | tf_op jit(solution)/shard_map/pallas_call | solution.py:587
  101.5 1.7 %shard_map.86 = (f32[1,1]{1,0:T(1,128)}, f32[128,256]{1,0:T(8,128)}, f32[40,256]{1,0:T(8,128)}) custom-call(f32[2,184,128]{2,1,0:T(8,128)} %shard_map.85.sums), custom_call_target="tpu_custom_call" | custom-call | tf_op jit(solution)/shard_map/pallas_call | solution.py:595

commit v5 on v4

--- a/solution.py
+++ b/solution.py
@@ -12,7 +12,7 @@
 PK = ROW // 3
 TALL, WIDE = 16 * ROW, N * ROW
 PAIR = T * ROW
-N_SEND, N_RECV = 92, 156
+N_SEND, N_RECV = 41, 63
 
 
 def ring(v, k):
@@ -32,7 +32,7 @@
         rep, node = lax.axis_index("rep"), lax.axis_index("nodes")
         self.z, self.y, self.x, self.c = rep // G, rep % G, node // T, node % T
         self.send_sem, self.recv_sem = send_sem, recv_sem
-        self.used, self.spare, self.ends = 0, [], []
+        self.used, self.ends = 0, []
 
     def dev(self, **place):
         z, y, x, c = (place.get(k, getattr(self, k)) for k in "zyxc")
@@ -45,8 +45,6 @@
         return self.dev(c=1 - self.c)
 
     def recv_index(self):
-        if self.spare:
-            return self.spare.pop()
         self.used += 1
         return self.used - 1
 
@@ -65,45 +63,36 @@
             copy.wait_send()
         self.ends = []
 
+    def places(self):
+        for j in range(G * G):
+            m = (j + 1) * 5 % (G * G)
+            yield ring(self.z, m // G), ring(self.y, m % G)
+
     def rep_each(self, src, buf):
         k, n = len(self.ends), self.used
-        self.used += G * G
+        self.used += G
         mine = buf.at[self.z, self.y]
         self.ends.append(self.copy(buf, buf, self.partner(), k, n))
-        for j in range(G * G):
-            m = (j + 1) * 5 % (G * G)
-            z, y = ring(self.z, m // G), ring(self.y, m % G)
-            self.copy(src, mine, self.dev(z=z, y=y, c=1 - self.c), k, n + m).start()
+        for j, (z, y) in enumerate(self.places()):
+            self.copy(src, mine, self.dev(z=z, y=y, c=1 - self.c), k, n + j // G).start()
 
         def each(fn):
             def body(j, _):
-                m = (j + 1) * 5 % (G * G)
-                self.copy(mine, mine, self.partner(), k, n + m).wait_recv()
-                fn(ring(self.z, -(m // G)), ring(self.y, -(m % G)))
+                self.copy(buf.at[0], buf.at[0], self.partner(), k, n + j).wait_recv()
+                for i in range(G):
+                    m = (j * G + i + 1) * 5 % (G * G)
+                    fn(ring(self.z, -(m // G)), ring(self.y, -(m % G)))
                 return _
 
-            lax.fori_loop(0, G * G, body, 0)
+            lax.fori_loop(0, G, body, 0)
 
         return each
 
-    def rep_all(self, src, buf):
-        k, n = len(self.ends), self.recv_index()
-        mine = buf.at[self.z, self.y]
-        whole = self.copy(buf, buf, self.partner(), k, n)
-        self.ends.append(whole)
-
-        def start(dz, dy):
-            z, y = ring(self.z, dz), ring(self.y, dy)
-            self.copy(src(z, y), mine, self.dev(z=z, y=y, c=1 - self.c), k, n).start()
-
-        return start, whole
-
     def rep_send(self, src, buf):
-        start, whole = self.rep_all(src, buf)
-        for j in range(G * G):
-            k = (j + 1) * 5 % (G * G)
-            start(k // G, k % G)
-        return whole
+        group = Group(self, buf)
+        for z, y in self.places():
+            group.send(src(z, y), buf.at[self.z, self.y], self.dev(z=z, y=y, c=1 - self.c))
+        return group
 
     def peers(self):
         out = [self.partner()]
@@ -113,30 +102,43 @@
         return out
 
 
+class Group:
+    def __init__(self, net, whole):
+        self.net, self.k, self.n = net, len(net.ends), net.recv_index()
+        self.all = net.copy(whole, whole, net.partner(), self.k, self.n)
+        net.ends.append(self.all)
+
+    def send(self, src, dst, device):
+        self.net.copy(src, dst, device, self.k, self.n).start()
+
+    def wait_recv(self):
+        self.all.wait_recv()
+
+
 class Tree:
-    def __init__(self, net, axis, at, far, near):
+    def __init__(self, net, axis, at, far, near, whole):
         self.net, self.at, self.far, self.near = net, at, far, near
         self.p = getattr(net, axis)
         self.side = net.near(axis, 1), net.near(axis, -1)
+        self.whole = whole
 
     def start(self):
         self.first = [self.net.send(self.at(ring(self.p, T), d), self.far(d), self.side[d]) for d in (0, 1)]
-        self.arrive = []
+        self.arrive = Group(self.net, self.whole)
 
     def free(self, d):
         t = ring(self.p, 1 - T * d)
-        self.arrive.append(self.net.send(self.at(t, 1 - d), self.near(d, 1 - d), self.side[d]))
+        self.arrive.send(self.at(t, 1 - d), self.near(d, 1 - d), self.side[d])
 
     def relay(self):
         for d in (0, 1):
             self.first[d].wait_recv()
             mine = self.at(ring(self.p, 1 - T * d), d)
             mine[...] = mine[...] + self.far(d)[...]
-            self.arrive.append(self.net.send(mine, self.near(d, d), self.side[d]))
+            self.arrive.send(mine, self.near(d, d), self.side[d])
 
     def end(self):
-        for copy in self.arrive:
-            copy.wait_recv()
+        self.arrive.wait_recv()
 
 
 class RepSum:
@@ -153,9 +155,10 @@
                 row = pl.ds((h * slices + s) * self.size + d * q, q)
                 return terms.at[t, :, row] if h else terms.at[:, t, row]
 
-            self.tree[h, s] = Tree(
-                net, "yz"[h], at, lambda d, h=h, s=s: far.at[h, s, d], lambda d, e, h=h, s=s: near.at[h, s, d, :, pl.ds(e * q, q)]
-            )
+            def part(d, e, h=h, s=s):
+                return near.at[h, s, d, :, pl.ds(e * q, q)]
+
+            self.tree[h, s] = Tree(net, "yz"[h], at, lambda d, h=h, s=s: far.at[h, s, d], part, near.at[h, s])
 
     def start(self, h):
         for s in self.slices:
@@ -178,9 +181,8 @@
             mid[...] = own + self.near[h, s, 0] + self.near[h, s, 1]
             axis = "zy"[h]
             arrivals.append(exchange(net, axis, lambda t: mid.at[t], self.last.at[h, s]))
-        for (h, s), copies in zip(self.parts, arrivals):
-            for copy in copies:
-                copy.wait_recv()
+        for (h, s), group in zip(self.parts, arrivals):
+            group.wait_recv()
             p = net.y if h else net.z
             total = self.mid[h, s, p]
             for k in (1, 2, 3):
@@ -190,7 +192,10 @@
 
 def exchange(net, axis, src, buf):
     p = getattr(net, axis)
-    return [net.send(src(ring(p, k)), buf.at[p], net.near(axis, k)) for k in (2, 1, 3)]
+    group = Group(net, buf.at[pl.ds(0, 3)])
+    for k in (2, 1, 3):
+        group.send(src(ring(p, k)), buf.at[p], net.near(axis, k))
+    return group
 
 
 def wait_all(copies):
@@ -199,14 +204,13 @@
 
 
 def gather_nodes(net, buf):
-    node = lambda k, core: ring(net.x, k) * T + core
-    mine = buf.at[node(0, net.c)]
-    other = 1 - net.c
-    out = []
+    mine = buf.at[net.x * T + net.c]
+    group = Group(net, buf.at[pl.ds(0, N - 1)])
     for k in (2, 1, 3):
-        out.append((node(-k, net.c), net.send(mine, mine, net.near("x", k))))
-        out.append((node(-k, other), net.send(mine, mine, net.dev(x=ring(net.x, k), c=other))))
-    return [(node(0, other), net.send(mine, mine, net.partner()))] + out
+        for core in (net.c, 1 - net.c):
+            group.send(mine, mine, net.dev(x=ring(net.x, k), c=core))
+    group.send(mine, mine, net.partner())
+    return group
 
 
 def gather_pairs(net, buf, done, extra):
@@ -234,13 +238,19 @@
 class Spread:
     def __init__(self, net, buf):
         self.net, self.buf = net, buf
-        self.first = [self.along(h, "yz"[h], net.z, net.y) for h in (0, 1)]
-        self.rest = [copy for h in (0, 1) for _, copy in self.along(h, "zy"[h], net.z, net.y)]
+        self.first = [[(k, net.send(ref, ref, device)) for k, ref, device in self.along(h, "yz"[h], net.z, net.y)] for h in (0, 1)]
+        self.rest = Group(net, buf.at[pl.ds(0, 3)])
+        for h in (0, 1):
+            self.cross(h, net.z, net.y)
 
     def along(self, h, axis, z, y):
         size = self.buf.shape[T] // T
         ref = self.buf.at[z, y, pl.ds(h * size, size)]
-        return [(k, self.net.send(ref, ref, self.net.near(axis, k))) for k in (2, 1, 3)]
+        return [(k, ref, self.net.near(axis, k)) for k in (2, 1, 3)]
+
+    def cross(self, h, z, y):
+        for _, ref, device in self.along(h, "zy"[h], z, y):
+            self.rest.send(ref, ref, device)
 
     def second(self):
         net = self.net
@@ -248,8 +258,7 @@
             for h in (0, 1):
                 k, copy = self.first[h][n]
                 copy.wait_recv()
-                z, y = (ring(net.z, -k), net.y) if h else (net.z, ring(net.y, -k))
-                self.rest += [copy for _, copy in self.along(h, "zy"[h], z, y)]
+                self.cross(h, ring(net.z, -k) if h else net.z, net.y if h else ring(net.y, -k))
 
 
 def lanes(shape):
@@ -267,17 +276,17 @@
 
 
 def scratch_shapes():
-    half, thin, piece = HID // T, ROW // 6, CLS + N
+    half, thin, piece = HID // T, ROW // G, CLS + N
     return dict(
         a_v=((G, G, ROW, WIDE), BF16),
         xg=((N, ROW, LANE), BF16),
         cg=((N, N, LANE), F32),
         y1=((WIDE, HID), BF16),
         zp=((G, G, ROW, HID), F32),
-        far=((T, 3, T, G, thin // T, HID), F32),
-        near=((T, 3, T, G, thin, HID), F32),
-        mid=((T, 3, G, thin, HID), F32),
-        last=((T, 3, G, thin, HID), F32),
+        far=((T, T, T, G, thin // T, HID), F32),
+        near=((T, T, T, G, thin, HID), F32),
+        mid=((T, T, G, thin, HID), F32),
+        last=((T, T, G, thin, HID), F32),
         z1=((ROW, HID), F32),
         h1=((ROW, HID), BF16),
         w2p=((LANE, HID), F32),
@@ -360,7 +369,7 @@
 
     def small_copies():
         swaps = [net.send(s[k], s[k + "_o"], net.partner()) for k in ("lab", "msk")]
-        return swaps + [copy for _, copy in gather_nodes(net, cg)]
+        return swaps + [gather_nodes(net, cg)]
 
     counts = gather_pairs(net, xg, y1_block, small_copies)
     for load in loads[small:]:
@@ -379,7 +388,6 @@
         else:
             zp[:, t, row] = term
 
-    base = net.used
     for k in (2, 1, 3, 0):
         for h, p in enumerate((y, z)):
             z1_block(h, ring(p, k))
@@ -389,7 +397,6 @@
                 sum1.free(h, k // T)
     z1 = s["z1"]
     sum1.finish(z1)
-    z1_used = list(range(base, net.used))
 
     h1 = s["h1"]
     h1[...] = jnp.maximum(z1[...], 0.0).astype(BF16)
@@ -409,7 +416,7 @@
         spread(y2g[j], y2u, j)
         return _
 
-    wait_all(counts + [copy for _, copy in blocks])
+    wait_all(counts + [blocks])
     lax.fori_loop(0, N, spread_y2, 0)
 
     zq, zi = s["zq"], s["zi"]
@@ -417,7 +424,7 @@
     at_count = lanes((PK, LANE)) == 3 * CLS
     count = jnp.where(at_count, jnp.broadcast_to(count, (PK, LANE)), 0.0)
 
-    start, arrivals = net.rep_all(lambda zz, yy: zq.at[zz, yy], zi)
+    arrivals = Group(net, zi)
 
     def z2_blocks(j, _):
         dz, p = j // T + 1, T * (j % T)
@@ -425,7 +432,7 @@
         term = dot(a_v[zz, pl.ds(p, T)].reshape(PAIR, WIDE), y2u[...], 1, 0)
         for k in (0, 1):
             zq[zz, p + k] = pack(term[k * ROW : (k + 1) * ROW]) + count
-            start(dz, p + k - y)
+            arrivals.send(zq.at[zz, p + k], zi.at[z, y], net.dev(z=zz, y=p + k, c=1 - c))
         return _
 
     lax.fori_loop(0, N, z2_blocks, 0)
@@ -434,7 +441,6 @@
     classes = lax.broadcasted_iota(jnp.int32, (LANE, ROW), 0)
     one_hot = (jnp.broadcast_to(label_row, (LANE, ROW)) == classes).astype(F32).T
     arrivals.wait_recv()
-    net.flush()
     packed = jnp.sum(zi[...].reshape(G * G, PK, LANE), axis=0)
 
     total = jnp.sum(jnp.where(at_count, packed, 0.0), axis=1, keepdims=True)
@@ -452,9 +458,7 @@
     g2s[...] = pack(g2).astype(BF16)
 
     arrivals = net.rep_each(g2s, g2g)
-    net.spare = z1_used
     masks.second()
-    net.spare = []
     arrivals(lambda zz, yy: spread(g2g[zz, yy], g2u, zz * G + yy))
 
     d2, d2i, d2s, d2t = (s[k] for k in ("d2", "d2i", "d2s", "d2t"))
@@ -467,15 +471,18 @@
         d2[T * k] = part[:, :PAIR]
         d2[T * k + 1] = part[:, PAIR:]
 
+    arrivals = Group(net, d2i.at[pl.ds(0, 3)])
+
     def d2_send(t):
-        return net.send(d2.at[t], d2i.at[x], net.dev(x=t, c=1 - c))
+        arrivals.send(d2.at[t], d2i.at[x], net.dev(x=t, c=1 - c))
 
     d2_block(1 - x // T)
-    copies = [d2_send(ring(x, T)), d2_send(3 - x)]
+    d2_send(ring(x, T))
+    d2_send(3 - x)
     d2_block(x // T)
-    copies.append(d2_send(x + 1 - T * (x % T)))
+    d2_send(x + 1 - T * (x % T))
     d2i[x] = d2[x]
-    wait_all(copies)
+    arrivals.wait_recv()
     d2s[c] = jnp.sum(d2i[...], axis=0)
     net.send(d2s.at[c], d2s.at[c], net.partner()).wait_recv()
     d2t[...] = jnp.concatenate([d2s[0] + d2s[1], jnp.zeros((LANE - CLS, PAIR), F32)], axis=0).T
@@ -492,10 +499,11 @@
         w2s[h, :CLS] = dw2_t[:, h * LANE : (h + 1) * LANE]
         w2s[h, CLS:] = loss_tile
     swap = net.send(w2s.at[1 - c], w2o, net.partner())
-    wait_all(masks.rest)
+    masks.rest.wait_recv()
     swap.wait_recv()
     wx[x] = w2s[c] + w2o[...]
     swaps = exchange(net, "x", lambda t: wx.at[x], wx)
+    net.flush()
 
     def g1_block(zz, yy):
         dy = jnp.concatenate(unpack(dyg[zz, yy].astype(F32)), axis=0).astype(BF16)
@@ -503,7 +511,6 @@
         g1g[zz, yy] = jnp.where(mg[zz, yy].astype(F32) > 0.0, dh1, 0.0).astype(BF16)
 
     arrivals(g1_block)
-    net.flush()
 
     e1, e1o, e1s, e1far, e1near = (s[k] for k in ("e1", "e1o", "e1s", "e1far", "e1near"))
     half = HID // T
@@ -511,7 +518,7 @@
 
     def tree_of(n):
         part = lambda d: pl.ds((T * n + d) * q, q)
-        return Tree(net, "x", lambda t, d: e1s.at[t, part(d)], lambda d: e1far.at[n, d], lambda d, e: e1near.at[d, part(e)])
+        return Tree(net, "x", lambda t, d: e1s.at[t, part(d)], lambda d: e1far.at[n, d], lambda d, e: e1near.at[d, part(e)], e1near.at[0])
 
     trees = [tree_of(n) for n in (0, 1)]
 
@@ -540,7 +547,7 @@
     e1_join(*own)
     for tree in trees:
         tree.relay()
-    wait_all(swaps)
+    swaps.wait_recv()
     wr_own = s["wr_own"]
     wr_own[...] = jnp.sum(wx[...], axis=0)
     w_arrivals = net.rep_send(lambda zz, yy: wr_own, wr)
@@ -557,7 +564,10 @@
     swap = net.send(wf.at[1 - c], wf.at[1 - c], net.partner())
     arrivals.wait_recv()
     rx[...] = jnp.sum(rai[...].reshape(G * G, N, LANE), axis=0)
-    wait_all([net.send(rx, rxi.at[x], net.dev(x=ring(x, k), c=1 - c)) for k in (2, 1, 3, 0)])
+    arrivals = Group(net, rxi)
+    for k in (2, 1, 3, 0):
+        arrivals.send(rx, rxi.at[x], net.dev(x=ring(x, k), c=1 - c))
+    arrivals.wait_recv()
     rs[...] = jnp.sum(rxi[...], axis=0)
     arrivals = net.rep_send(lambda zz, yy: rs, rf.at[c])
     swap.wait_recv()

time: 103 us -> 99.9 us (0.970)
  Pallas kernels: 103 us -> 99.1 us
    pallas_call x1, Pallas kernels: 101 us -> 97.4 us  [device_step(): pl.pallas_call(kernel, out_shape=struct(T, LANE + CLS + T * N, LANE), in_...]
where the time goes in v5:
time: 99.9 us; the launch traced here: 99.8 us
  Pallas kernels  99.1 us (99%)
    pallas_call x1, Pallas kernels, device_step(): pl.pallas_call(kernel, out_shape=struct(T, LANE + CLS + T * N, LANE), in_...  97.4 us

profile of v5, /device:TPU:1, one launch (start us, length us, event | category | flops | bytes accessed | tf_op | source)
XLA Modules:
  0.0 99.8 jit_solution(2772178254094961607)
XLA Ops:
  0.6 97.4 %shard_map.85.sums = f32[2,184,128]{2,1,0:T(8,128)} custom-call(bf16[4,4,192,1536]{3,2,1,0:T(8,128)(2,1)} %bitcast.4, bf16[192,128]{1,0:T(8,128)(2,1)} %x_ref.1, f32[128,256]{1,0:T(8,128)} %w1_ref.1, f32[40,256]{1,0:T(8,128)} %bitcast.5, s32[192]{0:T(256)} %lab_ref.1, s32[192]{0:T(256)} %msk_ref.1), custom_call_target="tpu_custom_call" | custom-call | tf_op jit(solution)/shard_map/pallas_call | solution.py:597
  98.1 1.7 %shard_map.86 = (f32[1,1]{1,0:T(1,128)}, f32[128,256]{1,0:T(8,128)}, f32[40,256]{1,0:T(8,128)}) custom-call(f32[2,184,128]{2,1,0:T(8,128)} %shard_map.85.sums), custom_call_target="tpu_custom_call" | custom-call | tf_op jit(solution)/shard_map/pallas_call | solution.py:605

commit v6 on v5

--- a/solution.py
+++ b/solution.py
@@ -12,7 +12,7 @@
 PK = ROW // 3
 TALL, WIDE = 16 * ROW, N * ROW
 PAIR = T * ROW
-N_SEND, N_RECV = 41, 63
+N_SEND, N_RECV = 41, 66
 
 
 def ring(v, k):
@@ -84,7 +84,8 @@
                     fn(ring(self.z, -(m // G)), ring(self.y, -(m % G)))
                 return _
 
-            lax.fori_loop(0, G, body, 0)
+            for j in range(G):
+                body(j, 0)
 
         return each
 
@@ -413,11 +414,12 @@
             dst[span(base * ROW + g * PK, PK)] = part.astype(BF16)
 
     def spread_y2(j, _):
-        spread(y2g[j], y2u, j)
+        for i in range(G):
+            spread(y2g[j * G + i], y2u, j * G + i)
         return _
 
     wait_all(counts + [blocks])
-    lax.fori_loop(0, N, spread_y2, 0)
+    lax.fori_loop(0, T, spread_y2, 0)
 
     zq, zi = s["zq"], s["zi"]
     count = jnp.sum(cg[...], axis=0)[:1]
@@ -569,12 +571,18 @@
         arrivals.send(rx, rxi.at[x], net.dev(x=ring(x, k), c=1 - c))
     arrivals.wait_recv()
     rs[...] = jnp.sum(rxi[...], axis=0)
-    arrivals = net.rep_send(lambda zz, yy: rs, rf.at[c])
+    mine = rf.at[c]
+    rf[c, z, y] = rs[...]
+    arrivals = net.rep_send(lambda zz, yy: rs, mine)
+    rows = [Group(net, mine.at[0]) for _ in range(3)] + [Group(net, mine.at[0, pl.ds(0, 3)])]
+    for j in range(G * G - 1):
+        m = (j + 1) * 5 % (G * G)
+        rows[m // G - 1].send(rs, mine.at[z, y], net.dev(z=ring(z, m // G), y=ring(y, m % G)))
     swap.wait_recv()
     out_ref[:, span(LANE, CLS + N)] = wf[...]
     out_ref[0, span(LANE + CLS + N, N)] = jnp.broadcast_to(total[:1], (N, LANE))
     arrivals.wait_recv()
-    net.send(rf.at[1 - c], rf.at[1 - c], net.partner()).wait_recv()
+    wait_all(rows)
     out_ref[:, :LANE] = rf[...].reshape(T, LANE, LANE)
     net.flush()
 

time: 99.9 us -> 98.3 us (0.984)
  Pallas kernels: 99.1 us -> 97.5 us
    pallas_call x1, Pallas kernels: 97.4 us -> 95.8 us  [device_step(): pl.pallas_call(kernel, out_shape=struct(T, LANE + CLS + T * N, LANE), in_...]
where the time goes in v6:
time: 98.3 us; the launch traced here: 98.2 us
  Pallas kernels  97.5 us (99%)
    pallas_call x1, Pallas kernels, device_step(): pl.pallas_call(kernel, out_shape=struct(T, LANE + CLS + T * N, LANE), in_...  95.8 us

profile of v6, /device:TPU:1, one launch (start us, length us, event | category | flops | bytes accessed | tf_op | source)
XLA Modules:
  0.0 98.2 jit_solution(14541885120490425166)
XLA Ops:
  0.6 95.8 %shard_map.85.sums = f32[2,184,128]{2,1,0:T(8,128)} custom-call(bf16[4,4,192,1536]{3,2,1,0:T(8,128)(2,1)} %bitcast.4, bf16[192,128]{1,0:T(8,128)(2,1)} %x_ref.1, f32[128,256]{1,0:T(8,128)} %w1_ref.1, f32[40,256]{1,0:T(8,128)} %bitcast.5, s32[192]{0:T(256)} %lab_ref.1, s32[192]{0:T(256)} %msk_ref.1), custom_call_target="tpu_custom_call" | custom-call | tf_op jit(solution)/shard_map/pallas_call | solution.py:605
  96.5 1.7 %shard_map.86 = (f32[1,1]{1,0:T(1,128)}, f32[128,256]{1,0:T(8,128)}, f32[40,256]{1,0:T(8,128)}) custom-call(f32[2,184,128]{2,1,0:T(8,128)} %shard_map.85.sums), custom_call_target="tpu_custom_call" | custom-call | tf_op jit(solution)/shard_map/pallas_call | solution.py:613

commit v7 on v6

--- a/solution.py
+++ b/solution.py
@@ -12,7 +12,7 @@
 PK = ROW // 3
 TALL, WIDE = 16 * ROW, N * ROW
 PAIR = T * ROW
-N_SEND, N_RECV = 41, 66
+N_SEND, N_RECV = 41, 63
 
 
 def ring(v, k):
@@ -204,8 +204,8 @@
         copy.wait_recv()
 
 
-def gather_nodes(net, buf):
-    mine = buf.at[net.x * T + net.c]
+def gather_nodes(net, buf, place=None):
+    mine = buf.at[net.x * T + net.c if place is None else place]
     group = Group(net, buf.at[pl.ds(0, N - 1)])
     for k in (2, 1, 3):
         for core in (net.c, 1 - net.c):
@@ -306,23 +306,20 @@
         mg=((G, G, ROW, HID), BF16),
         dys=((PK, LANE), BF16),
         dyg=((G, G, PK, LANE), BF16),
-        e1=((G, HID, PAIR), F32),
-        e1o=((G, half, PAIR), F32),
-        e1s=((G, half, PAIR), F32),
-        e1far=((T, T, half // G, PAIR), F32),
-        e1near=((T, half, PAIR), F32),
+        e1=((3, HID, WIDE // 3), F32),
+        e1o=((3, half, WIDE // 3), F32),
+        e1s=((3, half, WIDE // 3), F32),
+        e1far=((3, T, half // N, WIDE // 3), F32),
+        e1near=((3, T, half // G, WIDE // 3), F32),
         w2s=((T, piece, LANE), F32),
         w2o=((piece, LANE), F32),
         wx=((G, piece, LANE), F32),
         wr_own=((piece, LANE), F32),
         wr=((G, G, piece, LANE), F32),
         wf=((T, piece, LANE), F32),
-        ra=((G, G, N, LANE), F32),
-        rai=((G, G, N, LANE), F32),
-        rx=((N, LANE), F32),
-        rxi=((G, N, LANE), F32),
-        rs=((N, LANE), F32),
-        rf=((T, G, G, N, LANE), F32),
+        ra=((half // G, LANE), F32),
+        rai=((G, G, half // G, LANE), F32),
+        rf=((N, half // G, LANE), F32),
         w1v=((LANE, HID), F32),
         lab=((ROW,), jnp.int32),
         msk=((ROW,), jnp.int32),
@@ -515,74 +512,65 @@
     arrivals(g1_block)
 
     e1, e1o, e1s, e1far, e1near = (s[k] for k in ("e1", "e1o", "e1s", "e1far", "e1near"))
-    half = HID // T
-    q = half // G
+    half, size = HID // T, HID // N
+    q = size // T
 
     def tree_of(n):
-        part = lambda d: pl.ds((T * n + d) * q, q)
-        return Tree(net, "x", lambda t, d: e1s.at[t, part(d)], lambda d: e1far.at[n, d], lambda d, e: e1near.at[d, part(e)], e1near.at[0])
-
-    trees = [tree_of(n) for n in (0, 1)]
-
-    def e1_block(k):
-        t = ring(x, k)
-        e1[t] = dot(g1g[...].reshape(TALL, HID), a_cols(t, PAIR), 0, 0)
-        return t, net.send(e1.at[t, span((1 - c) * half, half)], e1o.at[t], net.partner())
-
-    def e1_join(t, copy):
+        part = lambda t, d: span(t * size + d * q, q)
+        at = lambda t, d: e1s.at[n, part(t, d)]
+        return Tree(net, "x", at, lambda d: e1far.at[n, d], lambda d, e: e1near.at[n, d, pl.ds(e * q, q)], e1near.at[n])
+
+    trees = [tree_of(n) for n in range(3)]
+    wide = WIDE // 3
+
+    def e1_block(n):
+        e1[n] = dot(g1g[...].reshape(TALL, HID), a_cols(n, wide), 0, 0)
+        return net.send(e1.at[n, span((1 - c) * half, half)], e1o.at[n], net.partner())
+
+    def e1_join(n, copy):
         copy.wait_recv()
-        e1s[t] = e1[t, span(c * half, half)] + e1o[t]
-
-    opposite = e1_block(2)
-    right = e1_block(1)
-    e1_join(*opposite)
-    for tree in trees:
-        tree.start()
-    left = e1_block(3)
-    e1_join(*right)
-    for tree in trees:
+        e1s[n] = e1[n, span(c * half, half)] + e1o[n]
+        trees[n].start()
+
+    def free(tree):
         tree.free(0)
-    own = e1_block(0)
-    e1_join(*left)
-    for tree in trees:
         tree.free(1)
-    e1_join(*own)
+
+    ahead = e1_block(0)
+    for n in (1, 2):
+        later = e1_block(n)
+        e1_join(n - 1, ahead)
+        ahead = later
+    free(trees[0])
+    e1_join(2, ahead)
+    free(trees[1])
+    free(trees[2])
     for tree in trees:
         tree.relay()
     swaps.wait_recv()
     wr_own = s["wr_own"]
     wr_own[...] = jnp.sum(wx[...], axis=0)
     w_arrivals = net.rep_send(lambda zz, yy: wr_own, wr)
-    for tree in trees:
+    dw1_t = []
+    for n, tree in enumerate(trees):
         tree.end()
-    dy1 = (e1s[x] + e1near[0] + e1near[1]).astype(BF16)
-    dw1_t = dot(dy1, xg[pl.ds(x * T, T)].reshape(PAIR, LANE), 1, 0)
-
-    ra, rai, rx, rxi, rs, rf = (s[k] for k in ("ra", "rai", "rx", "rxi", "rs", "rf"))
-    ra[...] = dw1_t.reshape(G, G, N, LANE)
-    arrivals = net.rep_send(lambda zz, yy: ra.at[zz, yy], rai)
+        dy1 = (e1s[n, span(x * size, size)] + e1near[n, 0] + e1near[n, 1]).astype(BF16)
+        dw1_t.append(dot(dy1, xg[...].reshape(WIDE, LANE)[n * wide : (n + 1) * wide], 1, 0))
+
+    ra, rai, rf = s["ra"], s["rai"], s["rf"]
+    ra[...] = dw1_t[0] + dw1_t[1] + dw1_t[2]
+    arrivals = net.rep_send(lambda zz, yy: ra, rai)
     w_arrivals.wait_recv()
     wf[1 - c] = jnp.sum(wr[...].reshape(G * G, CLS + N, LANE), axis=0)
     swap = net.send(wf.at[1 - c], wf.at[1 - c], net.partner())
     arrivals.wait_recv()
-    rx[...] = jnp.sum(rai[...].reshape(G * G, N, LANE), axis=0)
-    arrivals = Group(net, rxi)
-    for k in (2, 1, 3, 0):
-        arrivals.send(rx, rxi.at[x], net.dev(x=ring(x, k), c=1 - c))
-    arrivals.wait_recv()
-    rs[...] = jnp.sum(rxi[...], axis=0)
-    mine = rf.at[c]
-    rf[c, z, y] = rs[...]
-    arrivals = net.rep_send(lambda zz, yy: rs, mine)
-    rows = [Group(net, mine.at[0]) for _ in range(3)] + [Group(net, mine.at[0, pl.ds(0, 3)])]
-    for j in range(G * G - 1):
-        m = (j + 1) * 5 % (G * G)
-        rows[m // G - 1].send(rs, mine.at[z, y], net.dev(z=ring(z, m // G), y=ring(y, m % G)))
+    place = (1 - c) * G + x
+    rf[place] = jnp.sum(rai[...].reshape(G * G, size, LANE), axis=0)
+    arrivals = gather_nodes(net, rf, place)
     swap.wait_recv()
     out_ref[:, span(LANE, CLS + N)] = wf[...]
     out_ref[0, span(LANE + CLS + N, N)] = jnp.broadcast_to(total[:1], (N, LANE))
     arrivals.wait_recv()
-    wait_all(rows)
     out_ref[:, :LANE] = rf[...].reshape(T, LANE, LANE)
     net.flush()
 

time: 98.3 us -> 98 us (level)
  no operation moved by 1% of the time
where the time goes in v7:
time: 98 us; the launch traced here: 97.9 us
  Pallas kernels  97.2 us (99%)
    pallas_call x1, Pallas kernels, device_step(): pl.pallas_call(kernel, out_shape=struct(T, LANE + CLS + T * N, LANE), in_...  95.5 us

profile of v7, /device:TPU:1, one launch (start us, length us, event | category | flops | bytes accessed | tf_op | source)
XLA Modules:
  0.0 97.9 jit_solution(393946900389301994)
XLA Ops:
  0.6 95.5 %shard_map.85.sums = f32[2,184,128]{2,1,0:T(8,128)} custom-call(bf16[4,4,192,1536]{3,2,1,0:T(8,128)(2,1)} %bitcast.4, bf16[192,128]{1,0:T(8,128)(2,1)} %x_ref.1, f32[128,256]{1,0:T(8,128)} %w1_ref.1, f32[40,256]{1,0:T(8,128)} %bitcast.5, s32[192]{0:T(256)} %lab_ref.1, s32[192]{0:T(256)} %msk_ref.1), custom_call_target="tpu_custom_call" | custom-call | tf_op jit(solution)/shard_map/pallas_call | solution.py:593
  96.2 1.7 %shard_map.86 = (f32[1,1]{1,0:T(1,128)}, f32[128,256]{1,0:T(8,128)}, f32[40,256]{1,0:T(8,128)}) custom-call(f32[2,184,128]{2,1,0:T(8,128)} %shard_map.85.sums), custom_call_target="tpu_custom_call" | custom-call | tf_op jit(solution)/shard_map/pallas_call | solution.py:601

commit v8 on v7

--- a/solution.py
+++ b/solution.py
@@ -541,16 +541,17 @@
         later = e1_block(n)
         e1_join(n - 1, ahead)
         ahead = later
-    free(trees[0])
+        if n == 1:
+            free(trees[0])
     e1_join(2, ahead)
     free(trees[1])
     free(trees[2])
-    for tree in trees:
-        tree.relay()
     swaps.wait_recv()
     wr_own = s["wr_own"]
     wr_own[...] = jnp.sum(wx[...], axis=0)
     w_arrivals = net.rep_send(lambda zz, yy: wr_own, wr)
+    for tree in trees:
+        tree.relay()
     dw1_t = []
     for n, tree in enumerate(trees):
         tree.end()

time: 98 us -> 95.9 us (0.979)
  Pallas kernels: 97.2 us -> 95.2 us
    pallas_call x1, Pallas kernels: 95.5 us -> 93.4 us  [device_step(): pl.pallas_call(kernel, out_shape=struct(T, LANE + CLS + T * N, LANE), in_...]
where the time goes in v8:
time: 95.9 us; the launch traced here: 95.8 us
  Pallas kernels  95.2 us (99%)
    pallas_call x1, Pallas kernels, device_step(): pl.pallas_call(kernel, out_shape=struct(T, LANE + CLS + T * N, LANE), in_...  93.4 us

profile of v8, /device:TPU:1, one launch (start us, length us, event | category | flops | bytes accessed | tf_op | source)
XLA Modules:
  0.0 95.8 jit_solution(17004093269429896650)
XLA Ops:
  0.6 93.4 %shard_map.85.sums = f32[2,184,128]{2,1,0:T(8,128)} custom-call(bf16[4,4,192,1536]{3,2,1,0:T(8,128)(2,1)} %bitcast.4, bf16[192,128]{1,0:T(8,128)(2,1)} %x_ref.1, f32[128,256]{1,0:T(8,128)} %w1_ref.1, f32[40,256]{1,0:T(8,128)} %bitcast.5, s32[192]{0:T(256)} %lab_ref.1, s32[192]{0:T(256)} %msk_ref.1), custom_call_target="tpu_custom_call" | custom-call | tf_op jit(solution)/shard_map/pallas_call | solution.py:594
  94.1 1.7 %shard_map.86 = (f32[1,1]{1,0:T(1,128)}, f32[128,256]{1,0:T(8,128)}, f32[40,256]{1,0:T(8,128)}) custom-call(f32[2,184,128]{2,1,0:T(8,128)} %shard_map.85.sums), custom_call_target="tpu_custom_call" | custom-call | tf_op jit(solution)/shard_map/pallas_call | solution.py:602
